TPU v7x, 128 devices: a whole 4x4x4 slice. The times are simulated.
128 devices in a mesh: rows: 128 (over z, y, x, core).
Axes of the slice: x: 4, y: 4, z: 4, core: 2. Of those that a mesh axis runs over, the one named last changes fastest.
Arguments:
- events: float32 [4, 32, 1048576], P(None, None, 'rows'), may hold values from -8 to 8
- keep_indicator: int32 [4, 1048576], P(None, 'rows'), may hold values from 0 to 1, as said below
Outputs:
- lagging_mean: float32 [4, 32, 1048576], P(None, None, 'rows')
- deviation: float32 [4, 32, 1048576], P(None, None, 'rows')
Inputs may be any that keep to these rules, and one draw needn't show every extreme that they name: `keep_indicator`: in each table, each of the 128 aligned blocks of 8192 rows holds at least 4096 survivors, and some block holds exactly 4096.
All inputs are finite; a program needn't handle non-finite values.
Results may differ from a plain program's by a relative error of at most 0.0003.
Values sent between devices are 32-bit elements; how exact they have to be, the bound alone decides.
No kernel may reach another device: no remote copies, remote signals or barrier semaphores. Data moves between devices by JAX's collectives and lax.ppermute only.
A program may use at most 128 MiB of HBM per device.

v0:
```python
import jax
import jax.numpy as jnp
from jax import lax
from jax.experimental import pallas as pl
from jax.experimental.pallas import tpu as pltpu
from jax.sharding import Mesh
from jax.sharding import PartitionSpec as P


SPAN = 4096
LANES = 128
GROUP = 32
GROUP_SUM = 8
ROWS = ("rows_0", "rows_1", "rows_2", "rows_3")
SHAPE = (4, 4, 4, 2)
F32 = jnp.float32
I32 = jnp.int32
BF16 = jnp.bfloat16


def lanes_of(rows):
    return lax.broadcasted_iota(I32, (rows, LANES), 1)


def picked_lanes(values, index):
    return jnp.take_along_axis(values, index, axis=1, mode="promise_in_bounds")


def running_weights():
    row = lax.broadcasted_iota(I32, (2 * LANES, 2 * LANES), 0) & (LANES - 1)
    column = lax.broadcasted_iota(I32, (2 * LANES, 2 * LANES), 1)
    return ((row <= column) | (column >= LANES)).astype(F32).astype(BF16)


def index_tables(keep, flat, scalars, streams, tiles):
    count = streams * tiles
    for t in range(tiles):
        flat[t * streams : (t + 1) * streams, :] = keep[:, t * LANES : (t + 1) * LANES].astype(F32)
    flags = flat[...].astype(BF16)
    weights = running_weights()[:LANES]
    sums = jnp.dot(flags, weights, preferred_element_type=F32)
    within, total = (sums[:, :LANES], sums[:, LANES:])
    row = lax.broadcasted_iota(I32, (count, count), 0)
    column = lax.broadcasted_iota(I32, (count, count), 1)
    same = ((row ^ column) & (streams - 1)) == 0
    earlier = (same & (column < row)).astype(F32).astype(BF16)
    later = (same & (column > row)).astype(F32).astype(BF16)
    start = jnp.dot(earlier, total.astype(BF16), preferred_element_type=F32)
    line = lax.dot_general(
        jnp.ones((8, LANES), BF16), flags, (((1,), (1,)), ((), ())), preferred_element_type=F32
    )
    line_start = jnp.dot(line.astype(BF16), later, preferred_element_type=F32)
    sublane = lax.broadcasted_iota(I32, (8, count), 0)
    base = line_start + jnp.where(line == float(LANES), 1.0, 0.0)
    table = jnp.where(sublane == 0, line_start, jnp.where(sublane == 1, base, line_start + line))
    scalars[...] = table.astype(I32)
    begin = start.astype(I32)
    ordinal = ((lanes_of(count) - begin - 1) & (LANES - 1)).astype(F32)
    place = jnp.zeros((count, LANES), I32)
    step = LANES // 2
    while step:
        seen = picked_lanes(within, place + (step - 1))
        place = place + jnp.where(seen <= ordinal, step, 0)
        step //= 2
    return place, begin + within.astype(I32)


def pack_stream(s, streams, tiles, flat, state, index, starts, work, tail):
    features = state.shape[0]
    lane = lanes_of(features)
    weights = running_weights()
    work[:, 0:LANES] = jnp.zeros((features, LANES), F32)

    def step(g, carry):
        tiles_in = []
        for j in range(GROUP):
            at = pl.multiple_of((g * GROUP + j) * LANES, LANES)
            kept = flat[pl.ds((g * GROUP + j) * streams + s, 1), :]
            tiles_in.append(state[:, pl.ds(at, LANES)] * kept)
        values = jnp.concatenate(tiles_in, axis=0)
        high = values.astype(BF16)
        low = (values - high.astype(F32)).astype(BF16)
        sums = jnp.dot(
            jnp.concatenate([high, low], axis=1), weights, preferred_element_type=F32
        )
        for j in range(GROUP):
            t = g * GROUP + j
            at = pl.multiple_of(t * LANES, LANES)
            block = sums[j * features : (j + 1) * features]
            running = carry + block[:, :LANES]
            carry = carry + block[:, LANES:]
            state[:, pl.ds(at, LANES)] = running
            order = jnp.broadcast_to(index[pl.ds(t * streams + s, 1), :], (features, LANES))
            packed = picked_lanes(running, order)
            slot = starts[0, t * streams + s] + 1
            low_at = pl.multiple_of((slot >> 7) * LANES, LANES)
            pltpu.store(
                work.at[:, pl.ds(low_at, LANES)], packed, mask=lane >= (slot & (LANES - 1))
            )
            work[:, pl.ds(low_at + LANES, LANES)] = packed
        return carry

    total = lax.fori_loop(0, tiles // GROUP, step, jnp.zeros((features, LANES), F32))
    state[:, tiles * LANES : tiles * LANES + SPAN + LANES] = work[:, : SPAN + LANES]
    first = starts[2, (tiles - 1) * streams + s] - SPAN
    tile, shift = (first >> 7, first & (LANES - 1))
    turn = (LANES - shift) & (LANES - 1)
    from_first = lane < LANES - shift

    def turned(m):
        at = pl.multiple_of((tile + m) * LANES, LANES)
        return pltpu.roll(work[:, pl.ds(at, LANES)], turn, 1)

    before = turned(0)
    for m in range(SPAN // LANES):
        after = turned(m + 1)
        tail[:, m * LANES : (m + 1) * LANES] = jnp.where(from_first, before, after) - total
        before = after
    return total


def totals_line(s, total):
    features = total.shape[0]
    row = lax.broadcasted_iota(I32, (features, LANES), 0)
    chosen = jnp.where(lanes_of(features) == row + s * features, total, 0.0)
    return jnp.sum(chosen, axis=0, keepdims=True)


def pack_first_body(
    keep_hbm, events, state, flat, index, ranks, scalars, tail, totals,
    keep, starts, work, copied, loaded,
):
    streams, length = keep.shape
    features = events.shape[1]
    tiles = length // LANES
    loads = [
        pltpu.make_async_copy(events.at[s], state.at[s, :, pl.ds(0, length)], loaded.at[s])
        for s in range(streams)
    ]
    flags = pltpu.make_async_copy(keep_hbm, keep, copied)
    flags.start()
    for load in loads:
        load.start()
    flags.wait()
    index[...], ranks[...] = index_tables(keep, flat, scalars, streams, tiles)
    copy = pltpu.make_async_copy(scalars, starts, copied)
    copy.start()
    copy.wait()
    loads[0].wait()
    total = pack_stream(
        0, streams, tiles, flat, state.at[0], index, starts, work, tail.at[0]
    )
    for load in loads[1:]:
        load.wait()

    def step(g, sums):
        sums = list(sums)
        for j in range(GROUP_SUM):
            t = g * GROUP_SUM + j
            at = pl.multiple_of(t * LANES, LANES)
            for s in range(1, streams):
                kept = state[s, :, pl.ds(at, LANES)] * flat[pl.ds(t * streams + s, 1), :]
                sums[s - 1] = sums[s - 1] + kept
        return tuple(sums)

    zero = jnp.zeros((features, LANES), F32)
    sums = lax.fori_loop(0, tiles // GROUP_SUM, step, (zero,) * (streams - 1))
    sublane = lax.broadcasted_iota(I32, (8, LANES), 0)
    lane = lanes_of(8)
    counts = jnp.zeros((8, LANES), F32)
    for s in range(streams):
        counts = jnp.where(lane == s, starts[2, (tiles - 1) * streams + s].astype(F32), counts)
    line = totals_line(0, total)
    for s in range(1, streams):
        whole_sum = jnp.broadcast_to(
            jnp.sum(sums[s - 1], axis=1, keepdims=True), (features, LANES)
        )
        line = line + totals_line(s, whole_sum)
    line = jnp.broadcast_to(line, (8, LANES))
    totals[...] = jnp.where(sublane == 0, line, jnp.where(sublane == 1, counts, 0.0))


def spread_stream(s, at_stream, streams, length, starts, arrived, state, ranks, joint):
    features = state.shape[1]
    lane = lanes_of(features)
    joint[:, :SPAN] = jnp.where(lax.axis_index(ROWS) > 0, arrived[at_stream], 0.0)
    joint[:, SPAN:] = state[s, :, length : length + SPAN + LANES]

    def step(g, carry):
        for j in range(GROUP):
            t = g * GROUP + j
            row = t * streams + s
            at = pl.multiple_of(t * LANES, LANES)
            base = starts[1, row]
            low_at = pl.multiple_of((base >> 7) * LANES, LANES)
            window = jnp.where(
                lane >= (base & (LANES - 1)),
                joint[:, pl.ds(low_at, LANES)],
                joint[:, pl.ds(low_at + LANES, LANES)],
            )
            order = jnp.broadcast_to(ranks[pl.ds(row, 1), :] & (LANES - 1), (features, LANES))
            running = state[s, :, pl.ds(at, LANES)]
            state[s, :, pl.ds(length + at, LANES)] = (
                running - picked_lanes(window, order)
            ) * (1.0 / SPAN)
        return carry

    lax.fori_loop(0, length // LANES // GROUP, step, 0)


def means_of(s, length, state):
    return state.at[s, :, pl.ds(length, length)]


def gathered(totals_of):
    before = jnp.zeros(totals_of[0].shape, F32)
    number = 0
    for axis in reversed(ROWS):
        count, position = (lax.axis_size(axis), lax.axis_index(axis))
        if axis == ROWS[2]:
            for step in range(1, count):
                taken = (position + step >= count).astype(F32)
                before = before + totals_of[number][...] * taken
                number += 1
            continue
        bit = 1
        while bit < count:
            taken = ((position & bit) != 0).astype(F32)
            before = before + totals_of[number][...] * taken
            number += 1
            bit *= 2
    return before


IN_VMEM = pl.BlockSpec(memory_space=pltpu.VMEM)
IN_SMEM = pl.BlockSpec(memory_space=pltpu.SMEM)
IN_HBM = pl.BlockSpec(memory_space=pltpu.HBM)
PARAMS = pltpu.CompilerParams(vmem_limit_bytes=12 << 20)


def pack_first(keep, events):
    streams, features, length = events.shape
    count = streams * length // LANES
    shapes = [
        pltpu.VMEM((streams, features, 2 * length), F32),
        pltpu.VMEM((count, LANES), F32),
        pltpu.VMEM((count, LANES), I32),
        pltpu.VMEM((count, LANES), I32),
        pltpu.VMEM((8, count), I32),
        pltpu.VMEM((1, features, SPAN), F32),
        pltpu.VMEM((8, LANES), F32),
    ]
    return pl.pallas_call(
        pack_first_body,
        in_specs=[IN_HBM, IN_HBM],
        out_specs=[IN_VMEM] * len(shapes),
        out_shape=shapes,
        scratch_shapes=[
            pltpu.VMEM((streams, length), I32),
            pltpu.SMEM((8, count), I32),
            pltpu.VMEM((features, length + LANES), F32),
            pltpu.SemaphoreType.DMA,
            pltpu.SemaphoreType.DMA((streams,)),
        ],
        compiler_params=PARAMS,
        name="pack_first",
    )(
        pltpu.with_memory_space_constraint(keep, pltpu.HBM),
        pltpu.with_memory_space_constraint(events, pltpu.HBM),
    )


def pack(s, length, starts, flat, state, index, slot, number, shared=None):
    streams, features, _ = state.shape
    tiles = length // LANES

    def body(starts, flat, _, index, *refs):
        state, tail, work = refs[-3:]
        pack_stream(s, streams, tiles, flat, state.at[s], index, starts, work, tail.at[slot])

    given = [] if shared is None else [shared]
    return pl.pallas_call(
        body,
        in_specs=[IN_SMEM] + [IN_VMEM] * (3 + len(given)),
        out_specs=[IN_VMEM] * 2,
        out_shape=[
            pltpu.VMEM(state.shape, F32),
            pltpu.VMEM((number, features, SPAN), F32),
        ],
        scratch_shapes=[pltpu.VMEM((features, length + LANES), F32)],
        input_output_aliases={2: 0, **{4 + k: 1 for k in range(len(given))}},
        compiler_params=PARAMS,
        name="pack",
    )(starts, flat, state, index, *given)


def spread(s, at_stream, length, starts, arrived, state, ranks, lagging):
    streams, features, _ = state.shape

    def body(starts, arrived, _, ranks, *refs):
        *outs, joint, sent = refs[-4:] if s else (None,) + refs[-3:]
        state = outs[-2] if s else outs[-1]
        write = None
        if s:
            write = pltpu.make_async_copy(means_of(s - 1, length, state), outs[-1].at[s - 1], sent)
            write.start()
        spread_stream(s, at_stream, streams, length, starts, arrived, state, ranks, joint)
        if write is not None:
            write.wait()

    given = [] if lagging is None else [lagging]
    out_shape = [pltpu.VMEM(state.shape, F32)]
    if s:
        out_shape.append(jax.ShapeDtypeStruct((streams, features, length), F32))
    results = pl.pallas_call(
        body,
        in_specs=[IN_SMEM] + [IN_VMEM] * 3 + [IN_HBM] * len(given),
        out_specs=[IN_VMEM, IN_HBM][: len(out_shape)],
        out_shape=out_shape,
        scratch_shapes=[
            pltpu.VMEM((features, 2 * SPAN + LANES), F32),
            pltpu.SemaphoreType.DMA,
        ],
        input_output_aliases={2: 0, **{4 + k: 1 for k in range(len(given))}},
        compiler_params=PARAMS,
        name="spread",
    )(starts, arrived, state, ranks, *given)
    return (results[0], results[1] if s else None)


def finish(at_stream, length, starts, arrived, state, ranks, lagging, totals_of):
    streams, features, _ = state.shape
    last = streams - 1
    tiles = length // LANES
    count = ranks.shape[0]

    def body(starts, arrived, _, ranks, __, *refs):
        totals_of = refs[: len(refs) - 9]
        state, lagging, deviation, joint, columns, scale, staged, sent, gone = refs[-9:]
        writes = [
            pltpu.make_async_copy(
                means_of(last - 1, length, state), lagging.at[last - 1], sent.at[0]
            )
        ]
        writes[0].start()
        before = gathered(totals_of)
        sums = before[0:1, :]
        row = lax.broadcasted_iota(I32, (features, LANES), 0)
        for s in range(streams):
            chosen = jnp.where(lanes_of(features) == row + s * features, sums, 0.0)
            columns[s] = jnp.broadcast_to(
                jnp.sum(chosen, axis=1, keepdims=True), (features, LANES)
            )
        stream = lax.broadcasted_iota(I32, (count, LANES), 0) & (streams - 1)
        seen = jnp.zeros((count, LANES), F32)
        for s in range(streams):
            tally = jnp.sum(jnp.where(lanes_of(1) == s, before[1:2, :], 0.0))
            seen = jnp.where(stream == s, tally, seen)
        scale[...] = 1.0 / jnp.maximum(seen + ranks[...].astype(F32), 1.0)

        def deviate(s):
            column = columns[s]

            def step(g, carry):
                for j in range(GROUP):
                    t = g * GROUP + j
                    at = pl.multiple_of(t * LANES, LANES)
                    running = state[s, :, pl.ds(at, LANES)]
                    staged[s, :, pl.ds(at, LANES)] = state[s, :, pl.ds(length + at, LANES)] - (
                        column + running
                    ) * scale[pl.ds(t * streams + s, 1), :]
                return carry

            lax.fori_loop(0, tiles // GROUP, step, 0)
            write = pltpu.make_async_copy(staged.at[s], deviation.at[s], gone.at[s])
            write.start()
            writes.append(write)

        for s in range(last):
            deviate(s)
        spread_stream(last, at_stream, streams, length, starts, arrived, state, ranks, joint)
        write = pltpu.make_async_copy(means_of(last, length, state), lagging.at[last], sent.at[1])
        write.start()
        writes.append(write)
        deviate(last)
        for write in writes:
            write.wait()

    shape = jax.ShapeDtypeStruct((streams, features, length), F32)
    _, lagging, deviation = pl.pallas_call(
        body,
        in_specs=[IN_SMEM] + [IN_VMEM] * 3 + [IN_HBM] + [IN_VMEM] * len(totals_of),
        out_specs=[IN_VMEM, IN_HBM, IN_HBM],
        out_shape=[pltpu.VMEM(state.shape, F32), shape, shape],
        scratch_shapes=[
            pltpu.VMEM((features, 2 * SPAN + LANES), F32),
            pltpu.VMEM((streams, features, LANES), F32),
            pltpu.VMEM((count, LANES), F32),
            pltpu.VMEM((streams, features, length), F32),
            pltpu.SemaphoreType.DMA((2,)),
            pltpu.SemaphoreType.DMA((streams,)),
        ],
        input_output_aliases={2: 0, 4: 1},
        compiler_params=PARAMS,
        name="finish",
    )(starts, arrived, state, ranks, lagging, *totals_of)
    return (lagging, deviation)


def exchanged(totals):
    brought = []
    for axis in reversed(ROWS):
        count = lax.axis_size(axis)
        moving = totals
        bit = 1
        for _ in range(1, count):
            if axis == ROWS[2]:
                pairs = [(k, (k - 1) % count) for k in range(count)]
            elif bit < count:
                pairs = [(k, k ^ (2 * bit - 1)) for k in range(count)]
                moving = totals
                bit *= 2
            else:
                break
            moving = lax.ppermute(moving, axis, pairs)
            brought.append(moving)
            totals = totals + moving
    return brought


def from_behind(value):
    count = lax.axis_size(ROWS)
    return lax.ppermute(value, ROWS, [(k, (k + 1) % count) for k in range(count)])


def per_device(events, keep):
    streams, _, length = events.shape
    state, flat, index, ranks, starts, tail, totals = pack_first(keep, events)
    arrived = {0: (from_behind(tail), 0)}
    state, tail = pack(1, length, starts, flat, state, index, 0, 2)
    state, tail = pack(2, length, starts, flat, state, index, 1, 2, tail)
    there = from_behind(tail)
    arrived.update({1: (there, 0), 2: (there, 1)})
    state, tail = pack(3, length, starts, flat, state, index, 0, 1)
    arrived[3] = (from_behind(tail), 0)
    totals_of = exchanged(totals)
    lagging = None
    for s in range(streams - 1):
        there, k = arrived[s]
        state, lagging = spread(s, k, length, starts, there, state, ranks, lagging)
    there, k = arrived[streams - 1]
    return finish(k, length, starts, there, state, ranks, lagging, totals_of)


def solution(mesh):
    shape = SHAPE if mesh.size == 128 else (1, 1, mesh.size // 2, 2)
    finer = Mesh(mesh.devices.reshape(shape), ROWS)
    in_specs = (P(None, None, ROWS), P(None, ROWS))
    out_specs = (P(None, None, ROWS), P(None, None, ROWS))
    return jax.shard_map(
        per_device, mesh=finer, in_specs=in_specs, out_specs=out_specs, check_vma=False
    )
```

profile of v0, /device:TPU:6, one launch (start us, length us, event | category | flops | bytes accessed | tf_op | source)
XLA Modules:
  0.0 55.6 jit_solution(8046242258106783049)
XLA Ops:
  0.6 5.3 %pack_first.1 = (f32[4,32,16384]{2,1,0:T(8,128)S(1)}, f32[256,128]{1,0:T(8,128)S(1)}, s32[256,128]{1,0:T(8,128)S(1)}, s32[256,128]{1,0:T(8,128)S(1)}, s32[8,256]...) custom-call(s32[4,8192]{1,0:T(4,128)} %keep_hbm.1, f32[4,32,8192]{2,1,0:T(8,128)} %events.1), custom_call_target="tpu_custom_call" | custom-call | tf_op jit(solution)/shard_map/pack_first/pallas_call | solution.py:253
  5.9 2.1 %pack.3 = (f32[4,32,16384]{2,1,0:T(8,128)S(1)}, f32[2,32,4096]{2,1,0:T(8,128)S(1)}) custom-call(s32[8,256]{1,0:T(8,128)S(1)} %get-tuple-element.21.starts, f32[256,128]{1,0:T(8,128)S(1)} %get-tuple-element.22.flat, f32[4,32,16384]{2,1,0:T(8,128)S(1)} %get-tuple-element.23._, s32[256,128]{1,0:T(8,128)S(1)} %get-tuple-element.24.index), custom_call_target="tpu_custom_call", output_to_operand_aliasing={{0}: (2, {})} | custom-call | tf_op jit(solution)/shard_map/pack/pallas_call | solution.py:282
  8.0 2.1 %pack.4 = (f32[4,32,16384]{2,1,0:T(8,128)S(1)}, f32[2,32,4096]{2,1,0:T(8,128)S(1)}) custom-call(s32[8,256]{1,0:T(8,128)S(1)} %get-tuple-element.21.starts, f32[256,128]{1,0:T(8,128)S(1)} %get-tuple-element.22.flat, f32[4,32,16384]{2,1,0:T(8,128)S(1)} %get-tuple-element.25._, ...), custom_call_target="tpu_custom_call", output_to_operand_aliasing={{0}: (2, {}), {1}: (4, {})} | custom-call | tf_op jit(solution)/shard_map/pack/pallas_call | solution.py:282
  10.2 0.1 collective-permute-start.1
  10.2 1.6 %collective-permute-start.2 = (f32[1,32,4096]{2,1,0:T(8,128)S(1)}, f32[1,32,4096]{2,1,0:T(8,128)S(1)}, u32[]{:S(2)}, u32[]{:S(2)}) collective-permute-start(f32[1,32,4096]{2,1,0:T(8,128)S(1)} %get-tuple-element.30), channel_id=1, source_target_pairs={{0,1},{1,2},{2,3},{3,4},{4,5},{5,6},{6,7},{7,8},{8,9},{9,10},{10,1... | collective-permute-start | bytes 1572872 | tf_op jit(solution)/shard_map/ppermute | solution.py:433
  11.8 2.1 %pack.5 = (f32[4,32,16384]{2,1,0:T(8,128)S(1)}, f32[1,32,4096]{2,1,0:T(8,128)S(1)}) custom-call(s32[8,256]{1,0:T(8,128)S(1)} %get-tuple-element.21.starts, f32[256,128]{1,0:T(8,128)S(1)} %get-tuple-element.22.flat, f32[4,32,16384]{2,1,0:T(8,128)S(1)} %get-tuple-element.27._, s32[256,128]{1,0:T(8,128)S(1)} %get-tuple-element.24.index), custom_call_target="tpu_custom_call", output_to_operand_aliasing={{0}: (2, {})} | custom-call | tf_op jit(solution)/shard_map/pack/pallas_call | solution.py:282
  13.9 0.2 collective-permute-start
  14.1 1.5 %collective-permute-start.3 = (f32[8,128]{1,0:T(8,128)S(1)}, f32[8,128]{1,0:T(8,128)S(1)}, u32[]{:S(2)}, u32[]{:S(2)}) collective-permute-start(f32[8,128]{1,0:T(8,128)S(1)} %get-tuple-element.37), channel_id=1, source_target_pairs={{0,1},{1,0},{2,3},{3,2},{4,5},{5,4},{6,7},{7,6},{8,9},{9,8},{10,11... | collective-permute-start | bytes 12296 | tf_op jit(solution)/shard_map/ppermute | solution.py:425
  15.6 0.8 %collective-permute-done.3.refs_0_ = f32[8,128]{1,0:T(8,128)S(1)} collective-permute-done((f32[8,128]{1,0:T(8,128)S(1)}, f32[8,128]{1,0:T(8,128)S(1)}, u32[]{:S(2)}, u32[]{:S(2)}) %collective-permute-start.3) | collective-permute-done | bytes 4128 | tf_op jit(solution)/shard_map/ppermute | solution.py:425
  16.4 0.5 collective-permute-start.4
  17.0 4.3 %collective-permute-done.4.refs_1_ = f32[8,128]{1,0:T(8,128)S(1)} collective-permute-done((f32[8,128]{1,0:T(8,128)S(1)}, f32[8,128]{1,0:T(8,128)S(1)}, u32[]{:S(2)}, u32[]{:S(2)}) %collective-permute-start.4) | collective-permute-done | bytes 4128 | tf_op jit(solution)/shard_map/ppermute | solution.py:425
  21.2 0.0 collective-permute-start.5
  21.3 4.8 %collective-permute-done.5.refs_2_ = f32[8,128]{1,0:T(8,128)S(1)} collective-permute-done((f32[8,128]{1,0:T(8,128)S(1)}, f32[8,128]{1,0:T(8,128)S(1)}, u32[]{:S(2)}, u32[]{:S(2)}) %collective-permute-start.5) | collective-permute-done | bytes 4128 | tf_op jit(solution)/shard_map/ppermute | solution.py:425
  26.1 0.0 collective-permute-start.6
  26.1 4.8 %collective-permute-done.6.refs_3_ = f32[8,128]{1,0:T(8,128)S(1)} collective-permute-done((f32[8,128]{1,0:T(8,128)S(1)}, f32[8,128]{1,0:T(8,128)S(1)}, u32[]{:S(2)}, u32[]{:S(2)}) %collective-permute-start.6) | collective-permute-done | bytes 4128 | tf_op jit(solution)/shard_map/ppermute | solution.py:425
  30.9 1.6 %collective-permute-start.7 = (f32[8,128]{1,0:T(8,128)S(1)}, f32[8,128]{1,0:T(8,128)S(1)}, u32[]{:S(2)}, u32[]{:S(2)}) collective-permute-start(f32[8,128]{1,0:T(8,128)S(1)} %add_add_fusion), channel_id=1, source_target_pairs={{0,8},{8,0},{16,24},{24,16},{1,9},{9,1},{17,25},{25,17},{2,10},{10... | collective-permute-start | bytes 12296 | tf_op jit(solution)/shard_map/ppermute | solution.py:425
  32.5 2.0 %collective-permute-done.7.refs_4_ = f32[8,128]{1,0:T(8,128)S(1)} collective-permute-done((f32[8,128]{1,0:T(8,128)S(1)}, f32[8,128]{1,0:T(8,128)S(1)}, u32[]{:S(2)}, u32[]{:S(2)}) %collective-permute-start.7) | collective-permute-done | bytes 4128 | tf_op jit(solution)/shard_map/ppermute | solution.py:425
  34.5 3.0 %collective-permute-start.8 = (f32[8,128]{1,0:T(8,128)S(1)}, f32[8,128]{1,0:T(8,128)S(1)}, u32[]{:S(2)}, u32[]{:S(2)}) collective-permute-start(f32[8,128]{1,0:T(8,128)S(1)} %add.25), channel_id=1, source_target_pairs={{0,24},{8,16},{16,8},{24,0},{1,25},{9,17},{17,9},{25,1},{2,26},{10... | collective-permute-start | bytes 12296 | tf_op jit(solution)/shard_map/ppermute | solution.py:425
  37.5 1.8 %collective-permute-done.8.refs_5_ = f32[8,128]{1,0:T(8,128)S(1)} collective-permute-done((f32[8,128]{1,0:T(8,128)S(1)}, f32[8,128]{1,0:T(8,128)S(1)}, u32[]{:S(2)}, u32[]{:S(2)}) %collective-permute-start.8) | collective-permute-done | bytes 4128 | tf_op jit(solution)/shard_map/ppermute | solution.py:425
  39.3 1.9 %collective-permute-start.9 = (f32[8,128]{1,0:T(8,128)S(1)}, f32[8,128]{1,0:T(8,128)S(1)}, u32[]{:S(2)}, u32[]{:S(2)}) collective-permute-start(f32[8,128]{1,0:T(8,128)S(1)} %add.26), channel_id=1, source_target_pairs={{0,32},{32,0},{64,96},{96,64},{1,33},{33,1},{65,97},{97,65},{2,34}... | collective-permute-start | bytes 12296 | tf_op jit(solution)/shard_map/ppermute | solution.py:425
  41.2 1.7 %collective-permute-done.9.refs_6_ = f32[8,128]{1,0:T(8,128)S(1)} collective-permute-done((f32[8,128]{1,0:T(8,128)S(1)}, f32[8,128]{1,0:T(8,128)S(1)}, u32[]{:S(2)}, u32[]{:S(2)}) %collective-permute-start.9) | collective-permute-done | bytes 4128 | tf_op jit(solution)/shard_map/ppermute | solution.py:425
  42.9 4.0 %collective-permute-start.10 = (f32[8,128]{1,0:T(8,128)S(1)}, f32[8,128]{1,0:T(8,128)S(1)}, u32[]{:S(2)}, u32[]{:S(2)}) collective-permute-start(f32[8,128]{1,0:T(8,128)S(1)} %add.27), channel_id=1, source_target_pairs={{0,96},{32,64},{64,32},{96,0},{1,97},{33,65},{65,33},{97,1},{2,98}... | collective-permute-start | bytes 12296 | tf_op jit(solution)/shard_map/ppermute | solution.py:425
  47.0 0.0 collective-permute-done.2.arrived
  47.0 1.4 %spread.3._ = f32[4,32,16384]{2,1,0:T(8,128)S(1)} custom-call(s32[8,256]{1,0:T(8,128)S(1)} %get-tuple-element.21.starts, f32[1,32,4096]{2,1,0:T(8,128)S(1)} %collective-permute-done.2.arrived, f32[4,32,16384]{2,1,0:T(8,128)S(1)} %get-tuple-element.31._, s32[256,128]{1,0:T(8,128)S(1)} %get-tuple-element.32.ranks), custom_call_target="tpu_custom_call", output_to_operand_aliasing={{}: (2, {})} | custom-call | tf_op jit(solution)/shard_map/spread/pallas_call | solution.py:315
  48.4 0.0 collective-permute-done.1.arrived
  48.4 1.6 %spread.4 = (f32[4,32,16384]{2,1,0:T(8,128)S(1)}, f32[4,32,8192]{2,1,0:T(8,128)}) custom-call(s32[8,256]{1,0:T(8,128)S(1)} %get-tuple-element.21.starts, f32[2,32,4096]{2,1,0:T(8,128)S(1)} %collective-permute-done.1.arrived, f32[4,32,16384]{2,1,0:T(8,128)S(1)} %spread.3._, s32[256,128]{1,0:T(8,128)S(1)} %get-tuple-element.32.ranks), custom_call_target="tpu_custom_call", output_to_operand_aliasing={{0}: (2, {})} | custom-call | tf_op jit(solution)/shard_map/spread/pallas_call | solution.py:315
  50.1 1.7 %spread.5 = (f32[4,32,16384]{2,1,0:T(8,128)S(1)}, f32[4,32,8192]{2,1,0:T(8,128)}) custom-call(s32[8,256]{1,0:T(8,128)S(1)} %get-tuple-element.21.starts, f32[2,32,4096]{2,1,0:T(8,128)S(1)} %collective-permute-done.1.arrived, f32[4,32,16384]{2,1,0:T(8,128)S(1)} %get-tuple-element.33._, ...), custom_call_target="tpu_custom_call", output_to_operand_aliasing={{0}: (2, {}), {1}: (4, {})} | custom-call | tf_op jit(solution)/shard_map/spread/pallas_call | solution.py:315
  51.8 0.0 collective-permute-done.10.refs_7_
  51.8 0.0 collective-permute-done.arrived
  51.8 3.8 %finish.1 = (f32[4,32,16384]{2,1,0:T(8,128)S(1)}, f32[4,32,8192]{2,1,0:T(8,128)}, f32[4,32,8192]{2,1,0:T(8,128)}) custom-call(s32[8,256]{1,0:T(8,128)S(1)} %get-tuple-element.21.starts, f32[1,32,4096]{2,1,0:T(8,128)S(1)} %collective-permute-done.arrived, f32[4,32,16384]{2,1,0:T(8,128)S(1)} %get-tuple-element.35._, ...), custom_call_target="tpu_custom_call", output_to_operand_aliasing={{0}: (2, {}), {1}: (4, {})} | custom-call | tf_op jit(solution)/shard_map/finish/pallas_call | solution.py:390
  (5 shorter events, 0.0 us)
Async XLA Ops:
  10.2 38.3 %collective-permute-start.1 = (f32[2,32,4096]{2,1,0:T(8,128)S(1)}, f32[2,32,4096]{2,1,0:T(8,128)S(1)}, u32[]{:S(2)}, u32[]{:S(2)}) collective-permute-start(f32[2,32,4096]{2,1,0:T(8,128)S(1)} %get-tuple-element.29), channel_id=1, source_target_pairs={{0,1},{1,2},{2,3},{3,4},{4,5},{5,6},{6,7},{7,8},{8,9},{9,10},{10,1... | collective-permute-start | bytes 3145736 | tf_op jit(solution)/shard_map/ppermute | solution.py:433
  10.2 36.7 %collective-permute-start.2 = (f32[1,32,4096]{2,1,0:T(8,128)S(1)}, f32[1,32,4096]{2,1,0:T(8,128)S(1)}, u32[]{:S(2)}, u32[]{:S(2)}) collective-permute-start(f32[1,32,4096]{2,1,0:T(8,128)S(1)} %get-tuple-element.30), channel_id=1, source_target_pairs={{0,1},{1,2},{2,3},{3,4},{4,5},{5,6},{6,7},{7,8},{8,9},{9,10},{10,1... | collective-permute-start | bytes 1572872 | tf_op jit(solution)/shard_map/ppermute | solution.py:433
  13.9 37.8 %collective-permute-start = (f32[1,32,4096]{2,1,0:T(8,128)S(1)}, f32[1,32,4096]{2,1,0:T(8,128)S(1)}, u32[]{:S(2)}, u32[]{:S(2)}) collective-permute-start(f32[1,32,4096]{2,1,0:T(8,128)S(1)} %get-tuple-element.28), channel_id=1, source_target_pairs={{0,1},{1,2},{2,3},{3,4},{4,5},{5,6},{6,7},{7,8},{8,9},{9,10},{10,1... | collective-permute-start | bytes 1572872 | tf_op jit(solution)/shard_map/ppermute | solution.py:433
  14.1 2.3 %collective-permute-start.3 = (f32[8,128]{1,0:T(8,128)S(1)}, f32[8,128]{1,0:T(8,128)S(1)}, u32[]{:S(2)}, u32[]{:S(2)}) collective-permute-start(f32[8,128]{1,0:T(8,128)S(1)} %get-tuple-element.37), channel_id=1, source_target_pairs={{0,1},{1,0},{2,3},{3,2},{4,5},{5,4},{6,7},{7,6},{8,9},{9,8},{10,11... | collective-permute-start | bytes 12296 | tf_op jit(solution)/shard_map/ppermute | solution.py:425
  16.4 4.8 %collective-permute-start.4 = (f32[8,128]{1,0:T(8,128)S(1)}, f32[8,128]{1,0:T(8,128)S(1)}, u32[]{:S(2)}, u32[]{:S(2)}) collective-permute-start(f32[8,128]{1,0:T(8,128)S(1)} %add.21), channel_id=1, source_target_pairs={{0,6},{2,0},{4,2},{6,4},{1,7},{3,1},{5,3},{7,5},{8,14},{10,8},{12,... | collective-permute-start | bytes 12296 | tf_op jit(solution)/shard_map/ppermute | solution.py:425
  21.2 4.8 %collective-permute-start.5 = (f32[8,128]{1,0:T(8,128)S(1)}, f32[8,128]{1,0:T(8,128)S(1)}, u32[]{:S(2)}, u32[]{:S(2)}) collective-permute-start(f32[8,128]{1,0:T(8,128)S(1)} %collective-permute-done.4.refs_1_), channel_id=1, source_target_pairs={{0,6},{2,0},{4,2},{6,4},{1,7},{3,1},{5,3},{7,5},{8,14},{10,8},{12,... | collective-permute-start | bytes 12296 | tf_op jit(solution)/shard_map/ppermute | solution.py:425
  26.1 4.8 %collective-permute-start.6 = (f32[8,128]{1,0:T(8,128)S(1)}, f32[8,128]{1,0:T(8,128)S(1)}, u32[]{:S(2)}, u32[]{:S(2)}) collective-permute-start(f32[8,128]{1,0:T(8,128)S(1)} %collective-permute-done.5.refs_2_), channel_id=1, source_target_pairs={{0,6},{2,0},{4,2},{6,4},{1,7},{3,1},{5,3},{7,5},{8,14},{10,8},{12,... | collective-permute-start | bytes 12296 | tf_op jit(solution)/shard_map/ppermute | solution.py:425
  30.9 3.6 %collective-permute-start.7 = (f32[8,128]{1,0:T(8,128)S(1)}, f32[8,128]{1,0:T(8,128)S(1)}, u32[]{:S(2)}, u32[]{:S(2)}) collective-permute-start(f32[8,128]{1,0:T(8,128)S(1)} %add_add_fusion), channel_id=1, source_target_pairs={{0,8},{8,0},{16,24},{24,16},{1,9},{9,1},{17,25},{25,17},{2,10},{10... | collective-permute-start | bytes 12296 | tf_op jit(solution)/shard_map/ppermute | solution.py:425
  34.5 4.8 %collective-permute-start.8 = (f32[8,128]{1,0:T(8,128)S(1)}, f32[8,128]{1,0:T(8,128)S(1)}, u32[]{:S(2)}, u32[]{:S(2)}) collective-permute-start(f32[8,128]{1,0:T(8,128)S(1)} %add.25), channel_id=1, source_target_pairs={{0,24},{8,16},{16,8},{24,0},{1,25},{9,17},{17,9},{25,1},{2,26},{10... | collective-permute-start | bytes 12296 | tf_op jit(solution)/shard_map/ppermute | solution.py:425
  39.3 3.6 %collective-permute-start.9 = (f32[8,128]{1,0:T(8,128)S(1)}, f32[8,128]{1,0:T(8,128)S(1)}, u32[]{:S(2)}, u32[]{:S(2)}) collective-permute-start(f32[8,128]{1,0:T(8,128)S(1)} %add.26), channel_id=1, source_target_pairs={{0,32},{32,0},{64,96},{96,64},{1,33},{33,1},{65,97},{97,65},{2,34}... | collective-permute-start | bytes 12296 | tf_op jit(solution)/shard_map/ppermute | solution.py:425
  42.9 8.8 %collective-permute-start.10 = (f32[8,128]{1,0:T(8,128)S(1)}, f32[8,128]{1,0:T(8,128)S(1)}, u32[]{:S(2)}, u32[]{:S(2)}) collective-permute-start(f32[8,128]{1,0:T(8,128)S(1)} %add.27), channel_id=1, source_target_pairs={{0,96},{32,64},{64,32},{96,0},{1,97},{33,65},{65,33},{97,1},{2,98}... | collective-permute-start | bytes 12296 | tf_op jit(solution)/shard_map/ppermute | solution.py:425
where the time goes:
time: 55.7 us; the launch traced here: 55.6 us
  Pallas kernels  20.2 us (36%)
  waiting for transfers between devices  20.2 us (36%)
  starting transfers between devices  14.5 us (26%)
  between operations  0.72 us (1%)
    ppermute x8, waiting for transfers between devices, exchanged(): moving = lax.ppermute(moving, axis, pairs)  20.2 us
    ppermute x8, starting transfers between devices, exchanged(): moving = lax.ppermute(moving, axis, pairs)  12.6 us
    pallas_call x3, Pallas kernels, pack(): pl.pallas_call(body, in_specs=[IN_SMEM] + [IN_VMEM] * (3 + len(given)), o...  6.29 us
    pallas_call x1, Pallas kernels, pack_first(): pl.pallas_call(pack_first_body, in_specs=[IN_HBM, IN_HBM], out_specs=[IN_...  5.31 us
    pallas_call x3, Pallas kernels, spread(): pl.pallas_call(body, in_specs=[IN_SMEM] + [IN_VMEM] * 3 + [IN_HBM] * len(...  4.74 us
    pallas_call x1, Pallas kernels, finish(): pl.pallas_call(body, in_specs=[IN_SMEM] + [IN_VMEM] * 3 + [IN_HBM] + [IN_...  3.83 us
    ppermute x3, starting transfers between devices, from_behind(): lax.ppermute(value, ROWS, [(k, (k + 1) % count) for k in range(count)])  1.82 us
  transfers between devices with their start and end apart: 11, of which 7 were waited for; matrix products, arithmetic and copies ran while one was open for 0% of the time, Pallas kernels for 12%

commit v1 on v0

--- a/solution.py
+++ b/solution.py
@@ -212,24 +212,15 @@
     return state.at[s, :, pl.ds(length, length)]
 
 
-def gathered(totals_of):
-    before = jnp.zeros(totals_of[0].shape, F32)
-    number = 0
-    for axis in reversed(ROWS):
-        count, position = (lax.axis_size(axis), lax.axis_index(axis))
-        if axis == ROWS[2]:
-            for step in range(1, count):
-                taken = (position + step >= count).astype(F32)
-                before = before + totals_of[number][...] * taken
-                number += 1
-            continue
-        bit = 1
-        while bit < count:
-            taken = ((position & bit) != 0).astype(F32)
-            before = before + totals_of[number][...] * taken
-            number += 1
-            bit *= 2
-    return before
+def taken(axis, bit):
+    return ((lax.axis_index(axis) & bit) != 0).astype(F32)
+
+
+def earlier_rows(brought, axis):
+    number = len(brought)
+    return sum(
+        (brought[k][0:2, :] * taken(axis, 1 << k) for k in range(number)), jnp.zeros((2, LANES), F32)
+    )
 
 
 IN_VMEM = pl.BlockSpec(memory_space=pltpu.VMEM)
@@ -328,22 +319,44 @@
     return (results[0], results[1] if s else None)
 
 
-def finish(at_stream, length, starts, arrived, state, ranks, lagging, totals_of):
+def between(chip, brought):
+    counts = [len(brought[axis]) for axis in ROWS[:2]]
+
+    def body(chip, *refs):
+        *parts, out = refs
+        out[...] = jnp.zeros(out.shape, F32)
+        out[0:2, :] = chip[0:2, :]
+        out[2:4, :] = earlier_rows(parts[: counts[0]], ROWS[0]) + earlier_rows(
+            parts[counts[0] :], ROWS[1]
+        )
+
+    parts = [part for axis in ROWS[:2] for part in brought[axis]]
+    return pl.pallas_call(
+        body,
+        in_specs=[IN_VMEM] * (1 + len(parts)),
+        out_specs=IN_VMEM,
+        out_shape=pltpu.VMEM((8, LANES), F32),
+        compiler_params=PARAMS,
+        name="between",
+    )(chip, *parts)
+
+
+def finish(length, state, ranks, lagging, own, core, rows):
     streams, features, _ = state.shape
     last = streams - 1
     tiles = length // LANES
     count = ranks.shape[0]
 
-    def body(starts, arrived, _, ranks, __, *refs):
-        totals_of = refs[: len(refs) - 9]
-        state, lagging, deviation, joint, columns, scale, staged, sent, gone = refs[-9:]
+    def body(state, ranks, _, own, *refs):
+        core_parts, row_parts = (refs[: len(core)], refs[len(core) : len(refs) - 7])
+        lagging, deviation, columns, scale, staged, sent, gone = refs[-7:]
         writes = [
-            pltpu.make_async_copy(
-                means_of(last - 1, length, state), lagging.at[last - 1], sent.at[0]
-            )
+            pltpu.make_async_copy(means_of(last, length, state), lagging.at[last], sent)
         ]
         writes[0].start()
-        before = gathered(totals_of)
+        before = own[2:4, :] + earlier_rows(core_parts, ROWS[3]) + earlier_rows(row_parts, ROWS[2])
+        for part in row_parts:
+            before = before + part[2:4, :]
         sums = before[0:1, :]
         row = lax.broadcasted_iota(I32, (features, LANES), 0)
         for s in range(streams):
@@ -357,11 +370,10 @@
             tally = jnp.sum(jnp.where(lanes_of(1) == s, before[1:2, :], 0.0))
             seen = jnp.where(stream == s, tally, seen)
         scale[...] = 1.0 / jnp.maximum(seen + ranks[...].astype(F32), 1.0)
-
-        def deviate(s):
+        for s in range(streams):
             column = columns[s]
 
-            def step(g, carry):
+            def step(g, carry, s=s, column=column):
                 for j in range(GROUP):
                     t = g * GROUP + j
                     at = pl.multiple_of(t * LANES, LANES)
@@ -375,57 +387,38 @@
             write = pltpu.make_async_copy(staged.at[s], deviation.at[s], gone.at[s])
             write.start()
             writes.append(write)
-
-        for s in range(last):
-            deviate(s)
-        spread_stream(last, at_stream, streams, length, starts, arrived, state, ranks, joint)
-        write = pltpu.make_async_copy(means_of(last, length, state), lagging.at[last], sent.at[1])
-        write.start()
-        writes.append(write)
-        deviate(last)
         for write in writes:
             write.wait()
 
     shape = jax.ShapeDtypeStruct((streams, features, length), F32)
-    _, lagging, deviation = pl.pallas_call(
+    return pl.pallas_call(
         body,
-        in_specs=[IN_SMEM] + [IN_VMEM] * 3 + [IN_HBM] + [IN_VMEM] * len(totals_of),
-        out_specs=[IN_VMEM, IN_HBM, IN_HBM],
-        out_shape=[pltpu.VMEM(state.shape, F32), shape, shape],
+        in_specs=[IN_VMEM] * 2 + [IN_HBM] + [IN_VMEM] * (1 + len(core) + len(rows)),
+        out_specs=[IN_HBM, IN_HBM],
+        out_shape=[shape, shape],
         scratch_shapes=[
-            pltpu.VMEM((features, 2 * SPAN + LANES), F32),
             pltpu.VMEM((streams, features, LANES), F32),
             pltpu.VMEM((count, LANES), F32),
             pltpu.VMEM((streams, features, length), F32),
-            pltpu.SemaphoreType.DMA((2,)),
+            pltpu.SemaphoreType.DMA,
             pltpu.SemaphoreType.DMA((streams,)),
         ],
-        input_output_aliases={2: 0, 4: 1},
+        input_output_aliases={2: 0},
         compiler_params=PARAMS,
         name="finish",
-    )(starts, arrived, state, ranks, lagging, *totals_of)
-    return (lagging, deviation)
-
-
-def exchanged(totals):
+    )(state, ranks, lagging, own, *core, *rows)
+
+
+def exchanged(totals, axis):
+    count = lax.axis_size(axis)
     brought = []
-    for axis in reversed(ROWS):
-        count = lax.axis_size(axis)
-        moving = totals
-        bit = 1
-        for _ in range(1, count):
-            if axis == ROWS[2]:
-                pairs = [(k, (k - 1) % count) for k in range(count)]
-            elif bit < count:
-                pairs = [(k, k ^ (2 * bit - 1)) for k in range(count)]
-                moving = totals
-                bit *= 2
-            else:
-                break
-            moving = lax.ppermute(moving, axis, pairs)
-            brought.append(moving)
-            totals = totals + moving
-    return brought
+    bit = 1
+    while bit < count:
+        other = lax.ppermute(totals, axis, [(k, k ^ (2 * bit - 1)) for k in range(count)])
+        brought.append(other)
+        totals = totals + other
+        bit *= 2
+    return brought, totals
 
 
 def from_behind(value):
@@ -436,20 +429,23 @@
 def per_device(events, keep):
     streams, _, length = events.shape
     state, flat, index, ranks, starts, tail, totals = pack_first(keep, events)
-    arrived = {0: (from_behind(tail), 0)}
-    state, tail = pack(1, length, starts, flat, state, index, 0, 2)
-    state, tail = pack(2, length, starts, flat, state, index, 1, 2, tail)
-    there = from_behind(tail)
-    arrived.update({1: (there, 0), 2: (there, 1)})
-    state, tail = pack(3, length, starts, flat, state, index, 0, 1)
-    arrived[3] = (from_behind(tail), 0)
-    totals_of = exchanged(totals)
+    arrived = [from_behind(tail)]
+    for s in range(1, streams):
+        state, tail = pack(s, length, starts, flat, state, index, 0, 1)
+        arrived.append(from_behind(tail))
+    brought = {}
+    for axis in (ROWS[3], ROWS[1], ROWS[0]):
+        brought[axis], totals = exchanged(totals, axis)
+        if axis == ROWS[3]:
+            chip = totals
+    own = between(chip, brought)
+    rows, _ = exchanged(own, ROWS[2])
     lagging = None
-    for s in range(streams - 1):
-        there, k = arrived[s]
-        state, lagging = spread(s, k, length, starts, there, state, ranks, lagging)
-    there, k = arrived[streams - 1]
-    return finish(k, length, starts, there, state, ranks, lagging, totals_of)
+    for s in range(streams):
+        state, lagging = spread(s, 0, length, starts, arrived[s], state, ranks, lagging)
+    return tuple(
+        finish(length, state, ranks, lagging, own, brought[ROWS[3]], rows)
+    )
 
 
 def solution(mesh):

time: 55.7 us -> 50.6 us (0.908)
  the two profiles are of different devices: /device:TPU:6 before, /device:TPU:0 now
where the time goes in v1:
time: 50.6 us; the launch traced here: 50.5 us
  Pallas kernels  20.5 us (41%)
  starting transfers between devices  16.6 us (33%)
  waiting for transfers between devices  12.6 us (25%)
  between operations  0.74 us (1%)
    ppermute x7, starting transfers between devices, exchanged(): lax.ppermute(totals, axis, [(k, k ^ 2 * bit - 1) for k in range(count)])  13.1 us
    ppermute x7, waiting for transfers between devices, exchanged(): lax.ppermute(totals, axis, [(k, k ^ 2 * bit - 1) for k in range(count)])  12.6 us
    pallas_call x4, Pallas kernels, spread(): pl.pallas_call(body, in_specs=[IN_SMEM] + [IN_VMEM] * 3 + [IN_HBM] * len(...  6.38 us
    pallas_call x3, Pallas kernels, pack(): pl.pallas_call(body, in_specs=[IN_SMEM] + [IN_VMEM] * (3 + len(given)), o...  6.29 us
    pallas_call x1, Pallas kernels, pack_first(): pl.pallas_call(pack_first_body, in_specs=[IN_HBM, IN_HBM], out_specs=[IN_...  5.32 us
    ppermute x4, starting transfers between devices, from_behind(): lax.ppermute(value, ROWS, [(k, (k + 1) % count) for k in range(count)])  3.58 us
    pallas_call x1, Pallas kernels, finish(): pl.pallas_call(body, in_specs=[IN_VMEM] * 2 + [IN_HBM] + [IN_VMEM] * (1 +...  2.53 us
  transfers between devices with their start and end apart: 11, of which 6 were waited for; matrix products, arithmetic and copies ran while one was open for 0% of the time, Pallas kernels for 25%

profile of v1, /device:TPU:0, one launch (start us, length us, event | category | flops | bytes accessed | tf_op | source)
XLA Modules:
  0.0 50.5 jit_solution(1832830512248093918)
XLA Ops:
  0.6 5.3 %pack_first.1 = (f32[4,32,16384]{2,1,0:T(8,128)S(1)}, f32[256,128]{1,0:T(8,128)S(1)}, s32[256,128]{1,0:T(8,128)S(1)}, s32[256,128]{1,0:T(8,128)S(1)}, s32[8,256]...) custom-call(s32[4,8192]{1,0:T(4,128)} %keep_hbm.1, f32[4,32,8192]{2,1,0:T(8,128)} %events.1), custom_call_target="tpu_custom_call" | custom-call | tf_op jit(solution)/shard_map/pack_first/pallas_call | solution.py:244
  6.0 0.1 collective-permute-start.3
  6.0 2.1 %pack.3 = (f32[4,32,16384]{2,1,0:T(8,128)S(1)}, f32[1,32,4096]{2,1,0:T(8,128)S(1)}) custom-call(s32[8,256]{1,0:T(8,128)S(1)} %get-tuple-element.21.starts, f32[256,128]{1,0:T(8,128)S(1)} %get-tuple-element.22.flat, f32[4,32,16384]{2,1,0:T(8,128)S(1)} %get-tuple-element.23._, s32[256,128]{1,0:T(8,128)S(1)} %get-tuple-element.24.index), custom_call_target="tpu_custom_call", output_to_operand_aliasing={{0}: (2, {})} | custom-call | tf_op jit(solution)/shard_map/pack/pallas_call | solution.py:273
  8.1 1.8 %collective-permute-start.2 = (f32[1,32,4096]{2,1,0:T(8,128)S(1)}, f32[1,32,4096]{2,1,0:T(8,128)S(1)}, u32[]{:S(2)}, u32[]{:S(2)}) collective-permute-start(f32[1,32,4096]{2,1,0:T(8,128)S(1)} %get-tuple-element.29), channel_id=1, source_target_pairs={{0,1},{1,2},{2,3},{3,4},{4,5},{5,6},{6,7},{7,8},{8,9},{9,10},{10,1... | collective-permute-start | bytes 1572872 | tf_op jit(solution)/shard_map/ppermute | solution.py:426
  9.9 2.1 %pack.4 = (f32[4,32,16384]{2,1,0:T(8,128)S(1)}, f32[1,32,4096]{2,1,0:T(8,128)S(1)}) custom-call(s32[8,256]{1,0:T(8,128)S(1)} %get-tuple-element.21.starts, f32[256,128]{1,0:T(8,128)S(1)} %get-tuple-element.22.flat, f32[4,32,16384]{2,1,0:T(8,128)S(1)} %get-tuple-element.25._, s32[256,128]{1,0:T(8,128)S(1)} %get-tuple-element.24.index), custom_call_target="tpu_custom_call", output_to_operand_aliasing={{0}: (2, {})} | custom-call | tf_op jit(solution)/shard_map/pack/pallas_call | solution.py:273
  12.0 0.1 collective-permute-start.1
  12.1 2.1 %pack.5 = (f32[4,32,16384]{2,1,0:T(8,128)S(1)}, f32[1,32,4096]{2,1,0:T(8,128)S(1)}) custom-call(s32[8,256]{1,0:T(8,128)S(1)} %get-tuple-element.21.starts, f32[256,128]{1,0:T(8,128)S(1)} %get-tuple-element.22.flat, f32[4,32,16384]{2,1,0:T(8,128)S(1)} %get-tuple-element.26._, s32[256,128]{1,0:T(8,128)S(1)} %get-tuple-element.24.index), custom_call_target="tpu_custom_call", output_to_operand_aliasing={{0}: (2, {})} | custom-call | tf_op jit(solution)/shard_map/pack/pallas_call | solution.py:273
  14.2 1.6 %collective-permute-start = (f32[1,32,4096]{2,1,0:T(8,128)S(1)}, f32[1,32,4096]{2,1,0:T(8,128)S(1)}, u32[]{:S(2)}, u32[]{:S(2)}) collective-permute-start(f32[1,32,4096]{2,1,0:T(8,128)S(1)} %get-tuple-element.27), channel_id=1, source_target_pairs={{0,1},{1,2},{2,3},{3,4},{4,5},{5,6},{6,7},{7,8},{8,9},{9,10},{10,1... | collective-permute-start | bytes 1572872 | tf_op jit(solution)/shard_map/ppermute | solution.py:426
  15.8 0.1 collective-permute-start.4
  15.9 1.4 %collective-permute-done.4.refs_0_ = f32[8,128]{1,0:T(8,128)S(1)} collective-permute-done((f32[8,128]{1,0:T(8,128)S(1)}, f32[8,128]{1,0:T(8,128)S(1)}, u32[]{:S(2)}, u32[]{:S(2)}) %collective-permute-start.4) | collective-permute-done | bytes 4128 | tf_op jit(solution)/shard_map/ppermute | solution.py:417
  17.4 1.6 %collective-permute-start.5 = (f32[8,128]{1,0:T(8,128)S(1)}, f32[8,128]{1,0:T(8,128)S(1)}, u32[]{:S(2)}, u32[]{:S(2)}) collective-permute-start(f32[8,128]{1,0:T(8,128)S(1)} %add.15.chip), channel_id=1, source_target_pairs={{0,8},{8,0},{16,24},{24,16},{1,9},{9,1},{17,25},{25,17},{2,10},{10... | collective-permute-start | bytes 12296 | tf_op jit(solution)/shard_map/ppermute | solution.py:417
  19.0 2.0 %collective-permute-done.5.refs_2_ = f32[8,128]{1,0:T(8,128)S(1)} collective-permute-done((f32[8,128]{1,0:T(8,128)S(1)}, f32[8,128]{1,0:T(8,128)S(1)}, u32[]{:S(2)}, u32[]{:S(2)}) %collective-permute-start.5) | collective-permute-done | bytes 4128 | tf_op jit(solution)/shard_map/ppermute | solution.py:417
  21.0 3.4 %collective-permute-start.6 = (f32[8,128]{1,0:T(8,128)S(1)}, f32[8,128]{1,0:T(8,128)S(1)}, u32[]{:S(2)}, u32[]{:S(2)}) collective-permute-start(f32[8,128]{1,0:T(8,128)S(1)} %add.16), channel_id=1, source_target_pairs={{0,24},{8,16},{16,8},{24,0},{1,25},{9,17},{17,9},{25,1},{2,26},{10... | collective-permute-start | bytes 12296 | tf_op jit(solution)/shard_map/ppermute | solution.py:417
  24.4 1.9 %collective-permute-done.6.refs_3_ = f32[8,128]{1,0:T(8,128)S(1)} collective-permute-done((f32[8,128]{1,0:T(8,128)S(1)}, f32[8,128]{1,0:T(8,128)S(1)}, u32[]{:S(2)}, u32[]{:S(2)}) %collective-permute-start.6) | collective-permute-done | bytes 4128 | tf_op jit(solution)/shard_map/ppermute | solution.py:417
  26.3 1.9 %collective-permute-start.7 = (f32[8,128]{1,0:T(8,128)S(1)}, f32[8,128]{1,0:T(8,128)S(1)}, u32[]{:S(2)}, u32[]{:S(2)}) collective-permute-start(f32[8,128]{1,0:T(8,128)S(1)} %add.17), channel_id=1, source_target_pairs={{0,32},{32,0},{64,96},{96,64},{1,33},{33,1},{65,97},{97,65},{2,34}... | collective-permute-start | bytes 12296 | tf_op jit(solution)/shard_map/ppermute | solution.py:417
  28.2 1.7 %collective-permute-done.7.refs_0_ = f32[8,128]{1,0:T(8,128)S(1)} collective-permute-done((f32[8,128]{1,0:T(8,128)S(1)}, f32[8,128]{1,0:T(8,128)S(1)}, u32[]{:S(2)}, u32[]{:S(2)}) %collective-permute-start.7) | collective-permute-done | bytes 4128 | tf_op jit(solution)/shard_map/ppermute | solution.py:417
  29.9 4.4 %collective-permute-start.8 = (f32[8,128]{1,0:T(8,128)S(1)}, f32[8,128]{1,0:T(8,128)S(1)}, u32[]{:S(2)}, u32[]{:S(2)}) collective-permute-start(f32[8,128]{1,0:T(8,128)S(1)} %add.18), channel_id=1, source_target_pairs={{0,96},{32,64},{64,32},{96,0},{1,97},{33,65},{65,33},{97,1},{2,98}... | collective-permute-start | bytes 12296 | tf_op jit(solution)/shard_map/ppermute | solution.py:417
  34.3 1.9 %collective-permute-done.8.refs_1_ = f32[8,128]{1,0:T(8,128)S(1)} collective-permute-done((f32[8,128]{1,0:T(8,128)S(1)}, f32[8,128]{1,0:T(8,128)S(1)}, u32[]{:S(2)}, u32[]{:S(2)}) %collective-permute-start.8) | collective-permute-done | bytes 4128 | tf_op jit(solution)/shard_map/ppermute | solution.py:417
  36.2 0.2 collective-permute-start.9
  36.4 3.5 %collective-permute-done.9.refs_1_ = f32[8,128]{1,0:T(8,128)S(1)} collective-permute-done((f32[8,128]{1,0:T(8,128)S(1)}, f32[8,128]{1,0:T(8,128)S(1)}, u32[]{:S(2)}, u32[]{:S(2)}) %collective-permute-start.9) | collective-permute-done | bytes 4128 | tf_op jit(solution)/shard_map/ppermute | solution.py:417
  39.9 1.6 %collective-permute-start.10 = (f32[8,128]{1,0:T(8,128)S(1)}, f32[8,128]{1,0:T(8,128)S(1)}, u32[]{:S(2)}, u32[]{:S(2)}) collective-permute-start(f32[8,128]{1,0:T(8,128)S(1)} %add.19), channel_id=1, source_target_pairs={{0,6},{2,4},{4,2},{6,0},{1,7},{3,5},{5,3},{7,1},{8,14},{10,12},{12... | collective-permute-start | bytes 12296 | tf_op jit(solution)/shard_map/ppermute | solution.py:417
  41.5 0.0 collective-permute-done.3.arrived
  41.5 1.4 %spread.4._ = f32[4,32,16384]{2,1,0:T(8,128)S(1)} custom-call(s32[8,256]{1,0:T(8,128)S(1)} %get-tuple-element.21.starts, f32[1,32,4096]{2,1,0:T(8,128)S(1)} %collective-permute-done.3.arrived, f32[4,32,16384]{2,1,0:T(8,128)S(1)} %get-tuple-element.31._, s32[256,128]{1,0:T(8,128)S(1)} %get-tuple-element.32.ranks), custom_call_target="tpu_custom_call", output_to_operand_aliasing={{}: (2, {})} | custom-call | tf_op jit(solution)/shard_map/spread/pallas_call | solution.py:306
  43.0 0.0 collective-permute-done.2.arrived
  43.0 1.6 %spread.5 = (f32[4,32,16384]{2,1,0:T(8,128)S(1)}, f32[4,32,8192]{2,1,0:T(8,128)}) custom-call(s32[8,256]{1,0:T(8,128)S(1)} %get-tuple-element.21.starts, f32[1,32,4096]{2,1,0:T(8,128)S(1)} %collective-permute-done.2.arrived, f32[4,32,16384]{2,1,0:T(8,128)S(1)} %spread.4._, s32[256,128]{1,0:T(8,128)S(1)} %get-tuple-element.32.ranks), custom_call_target="tpu_custom_call", output_to_operand_aliasing={{0}: (2, {})} | custom-call | tf_op jit(solution)/shard_map/spread/pallas_call | solution.py:306
  44.6 0.0 collective-permute-done.1.arrived
  44.6 1.7 %spread.6 = (f32[4,32,16384]{2,1,0:T(8,128)S(1)}, f32[4,32,8192]{2,1,0:T(8,128)}) custom-call(s32[8,256]{1,0:T(8,128)S(1)} %get-tuple-element.21.starts, f32[1,32,4096]{2,1,0:T(8,128)S(1)} %collective-permute-done.1.arrived, f32[4,32,16384]{2,1,0:T(8,128)S(1)} %get-tuple-element.33._, ...), custom_call_target="tpu_custom_call", output_to_operand_aliasing={{0}: (2, {}), {1}: (4, {})} | custom-call | tf_op jit(solution)/shard_map/spread/pallas_call | solution.py:306
  46.3 0.0 collective-permute-done.arrived
  46.3 1.7 %spread.7 = (f32[4,32,16384]{2,1,0:T(8,128)S(1)}, f32[4,32,8192]{2,1,0:T(8,128)}) custom-call(s32[8,256]{1,0:T(8,128)S(1)} %get-tuple-element.21.starts, f32[1,32,4096]{2,1,0:T(8,128)S(1)} %collective-permute-done.arrived, f32[4,32,16384]{2,1,0:T(8,128)S(1)} %get-tuple-element.35._, ...), custom_call_target="tpu_custom_call", output_to_operand_aliasing={{0}: (2, {}), {1}: (4, {})} | custom-call | tf_op jit(solution)/shard_map/spread/pallas_call | solution.py:306
  48.0 0.0 collective-permute-done.10.refs_2_
  48.0 2.5 %finish.1 = (f32[4,32,8192]{2,1,0:T(8,128)}, f32[4,32,8192]{2,1,0:T(8,128)}) custom-call(f32[4,32,16384]{2,1,0:T(8,128)S(1)} %get-tuple-element.37.state, s32[256,128]{1,0:T(8,128)S(1)} %get-tuple-element.32.ranks, f32[4,32,8192]{2,1,0:T(8,128)} %get-tuple-element.38._, f32[8,128]{1,0:T(8,128)S(1)} %between.1.own, ...), custom_call_target="tpu_custom_call", output_to_operand_aliasing={{0}: (2, {})} | custom-call | tf_op jit(solution)/shard_map/finish/pallas_call | solution.py:394
  (6 shorter events, 0.0 us)
Async XLA Ops:
  6.0 35.6 %collective-permute-start.3 = (f32[1,32,4096]{2,1,0:T(8,128)S(1)}, f32[1,32,4096]{2,1,0:T(8,128)S(1)}, u32[]{:S(2)}, u32[]{:S(2)}) collective-permute-start(f32[1,32,4096]{2,1,0:T(8,128)S(1)} %get-tuple-element.30), channel_id=1, source_target_pairs={{0,1},{1,2},{2,3},{3,4},{4,5},{5,6},{6,7},{7,8},{8,9},{9,10},{10,1... | collective-permute-start | bytes 1572872 | tf_op jit(solution)/shard_map/ppermute | solution.py:426
  8.1 34.8 %collective-permute-start.2 = (f32[1,32,4096]{2,1,0:T(8,128)S(1)}, f32[1,32,4096]{2,1,0:T(8,128)S(1)}, u32[]{:S(2)}, u32[]{:S(2)}) collective-permute-start(f32[1,32,4096]{2,1,0:T(8,128)S(1)} %get-tuple-element.29), channel_id=1, source_target_pairs={{0,1},{1,2},{2,3},{3,4},{4,5},{5,6},{6,7},{7,8},{8,9},{9,10},{10,1... | collective-permute-start | bytes 1572872 | tf_op jit(solution)/shard_map/ppermute | solution.py:426
  12.0 32.6 %collective-permute-start.1 = (f32[1,32,4096]{2,1,0:T(8,128)S(1)}, f32[1,32,4096]{2,1,0:T(8,128)S(1)}, u32[]{:S(2)}, u32[]{:S(2)}) collective-permute-start(f32[1,32,4096]{2,1,0:T(8,128)S(1)} %get-tuple-element.28), channel_id=1, source_target_pairs={{0,1},{1,2},{2,3},{3,4},{4,5},{5,6},{6,7},{7,8},{8,9},{9,10},{10,1... | collective-permute-start | bytes 1572872 | tf_op jit(solution)/shard_map/ppermute | solution.py:426
  14.2 32.1 %collective-permute-start = (f32[1,32,4096]{2,1,0:T(8,128)S(1)}, f32[1,32,4096]{2,1,0:T(8,128)S(1)}, u32[]{:S(2)}, u32[]{:S(2)}) collective-permute-start(f32[1,32,4096]{2,1,0:T(8,128)S(1)} %get-tuple-element.27), channel_id=1, source_target_pairs={{0,1},{1,2},{2,3},{3,4},{4,5},{5,6},{6,7},{7,8},{8,9},{9,10},{10,1... | collective-permute-start | bytes 1572872 | tf_op jit(solution)/shard_map/ppermute | solution.py:426
  15.8 1.5 %collective-permute-start.4 = (f32[8,128]{1,0:T(8,128)S(1)}, f32[8,128]{1,0:T(8,128)S(1)}, u32[]{:S(2)}, u32[]{:S(2)}) collective-permute-start(f32[8,128]{1,0:T(8,128)S(1)} %get-tuple-element.39), channel_id=1, source_target_pairs={{0,1},{1,0},{2,3},{3,2},{4,5},{5,4},{6,7},{7,6},{8,9},{9,8},{10,11... | collective-permute-start | bytes 12296 | tf_op jit(solution)/shard_map/ppermute | solution.py:417
  17.4 3.6 %collective-permute-start.5 = (f32[8,128]{1,0:T(8,128)S(1)}, f32[8,128]{1,0:T(8,128)S(1)}, u32[]{:S(2)}, u32[]{:S(2)}) collective-permute-start(f32[8,128]{1,0:T(8,128)S(1)} %add.15.chip), channel_id=1, source_target_pairs={{0,8},{8,0},{16,24},{24,16},{1,9},{9,1},{17,25},{25,17},{2,10},{10... | collective-permute-start | bytes 12296 | tf_op jit(solution)/shard_map/ppermute | solution.py:417
  21.0 5.3 %collective-permute-start.6 = (f32[8,128]{1,0:T(8,128)S(1)}, f32[8,128]{1,0:T(8,128)S(1)}, u32[]{:S(2)}, u32[]{:S(2)}) collective-permute-start(f32[8,128]{1,0:T(8,128)S(1)} %add.16), channel_id=1, source_target_pairs={{0,24},{8,16},{16,8},{24,0},{1,25},{9,17},{17,9},{25,1},{2,26},{10... | collective-permute-start | bytes 12296 | tf_op jit(solution)/shard_map/ppermute | solution.py:417
  26.3 3.6 %collective-permute-start.7 = (f32[8,128]{1,0:T(8,128)S(1)}, f32[8,128]{1,0:T(8,128)S(1)}, u32[]{:S(2)}, u32[]{:S(2)}) collective-permute-start(f32[8,128]{1,0:T(8,128)S(1)} %add.17), channel_id=1, source_target_pairs={{0,32},{32,0},{64,96},{96,64},{1,33},{33,1},{65,97},{97,65},{2,34}... | collective-permute-start | bytes 12296 | tf_op jit(solution)/shard_map/ppermute | solution.py:417
  29.9 6.3 %collective-permute-start.8 = (f32[8,128]{1,0:T(8,128)S(1)}, f32[8,128]{1,0:T(8,128)S(1)}, u32[]{:S(2)}, u32[]{:S(2)}) collective-permute-start(f32[8,128]{1,0:T(8,128)S(1)} %add.18), channel_id=1, source_target_pairs={{0,96},{32,64},{64,32},{96,0},{1,97},{33,65},{65,33},{97,1},{2,98}... | collective-permute-start | bytes 12296 | tf_op jit(solution)/shard_map/ppermute | solution.py:417
  36.2 3.7 %collective-permute-start.9 = (f32[8,128]{1,0:T(8,128)S(1)}, f32[8,128]{1,0:T(8,128)S(1)}, u32[]{:S(2)}, u32[]{:S(2)}) collective-permute-start(f32[8,128]{1,0:T(8,128)S(1)} %between.1.own), channel_id=1, source_target_pairs={{0,2},{2,0},{4,6},{6,4},{1,3},{3,1},{5,7},{7,5},{8,10},{10,8},{12,... | collective-permute-start | bytes 12296 | tf_op jit(solution)/shard_map/ppermute | solution.py:417
  39.9 8.1 %collective-permute-start.10 = (f32[8,128]{1,0:T(8,128)S(1)}, f32[8,128]{1,0:T(8,128)S(1)}, u32[]{:S(2)}, u32[]{:S(2)}) collective-permute-start(f32[8,128]{1,0:T(8,128)S(1)} %add.19), channel_id=1, source_target_pairs={{0,6},{2,4},{4,2},{6,0},{1,7},{3,5},{5,3},{7,1},{8,14},{10,12},{12... | collective-permute-start | bytes 12296 | tf_op jit(solution)/shard_map/ppermute | solution.py:417

commit v2 on v1

--- a/solution.py
+++ b/solution.py
@@ -9,8 +9,8 @@
 
 SPAN = 4096
 LANES = 128
-GROUP = 32
-GROUP_SUM = 8
+GROUP = 64
+GROUP_SUM = 16
 ROWS = ("rows_0", "rows_1", "rows_2", "rows_3")
 SHAPE = (4, 4, 4, 2)
 F32 = jnp.float32
@@ -32,7 +32,7 @@
     return ((row <= column) | (column >= LANES)).astype(F32).astype(BF16)
 
 
-def index_tables(keep, flat, scalars, streams, tiles):
+def index_tables(keep, flat, scalars, copy, streams, tiles):
     count = streams * tiles
     for t in range(tiles):
         flat[t * streams : (t + 1) * streams, :] = keep[:, t * LANES : (t + 1) * LANES].astype(F32)
@@ -54,15 +54,18 @@
     base = line_start + jnp.where(line == float(LANES), 1.0, 0.0)
     table = jnp.where(sublane == 0, line_start, jnp.where(sublane == 1, base, line_start + line))
     scalars[...] = table.astype(I32)
+    copy.start()
+    ordinal = lanes_of(count).astype(F32)
+    place = jnp.zeros((count, LANES), I32)
+    for step, times in ((32, 3), (8, 3), (2, 3), (1, 1)):
+        found = place
+        for k in range(1, times + 1):
+            seen = picked_lanes(within, place + (k * step - 1))
+            found = found + jnp.where(seen <= ordinal, step, 0)
+        place = found
     begin = start.astype(I32)
-    ordinal = ((lanes_of(count) - begin - 1) & (LANES - 1)).astype(F32)
-    place = jnp.zeros((count, LANES), I32)
-    step = LANES // 2
-    while step:
-        seen = picked_lanes(within, place + (step - 1))
-        place = place + jnp.where(seen <= ordinal, step, 0)
-        step //= 2
-    return place, begin + within.astype(I32)
+    turned = picked_lanes(place, (lanes_of(count) - begin - 1) & (LANES - 1))
+    return turned, begin + within.astype(I32)
 
 
 def pack_stream(s, streams, tiles, flat, state, index, starts, work, tail):
@@ -127,8 +130,8 @@
 
 
 def pack_first_body(
-    keep_hbm, events, state, flat, index, ranks, scalars, tail, totals,
-    keep, starts, work, copied, loaded,
+    keep_hbm, events, state, flat, index, ranks, starts, tail, totals,
+    keep, scalars, work, copied, loaded,
 ):
     streams, length = keep.shape
     features = events.shape[1]
@@ -139,12 +142,12 @@
     ]
     flags = pltpu.make_async_copy(keep_hbm, keep, copied)
     flags.start()
-    for load in loads:
+    loads[0].start()
+    flags.wait()
+    for load in loads[1:]:
         load.start()
-    flags.wait()
-    index[...], ranks[...] = index_tables(keep, flat, scalars, streams, tiles)
     copy = pltpu.make_async_copy(scalars, starts, copied)
-    copy.start()
+    index[...], ranks[...] = index_tables(keep, flat, scalars, copy, streams, tiles)
     copy.wait()
     loads[0].wait()
     total = pack_stream(
@@ -237,18 +240,18 @@
         pltpu.VMEM((count, LANES), F32),
         pltpu.VMEM((count, LANES), I32),
         pltpu.VMEM((count, LANES), I32),
-        pltpu.VMEM((8, count), I32),
+        pltpu.SMEM((8, count), I32),
         pltpu.VMEM((1, features, SPAN), F32),
         pltpu.VMEM((8, LANES), F32),
     ]
     return pl.pallas_call(
         pack_first_body,
         in_specs=[IN_HBM, IN_HBM],
-        out_specs=[IN_VMEM] * len(shapes),
+        out_specs=[IN_VMEM] * 4 + [IN_SMEM] + [IN_VMEM] * 2,
         out_shape=shapes,
         scratch_shapes=[
             pltpu.VMEM((streams, length), I32),
-            pltpu.SMEM((8, count), I32),
+            pltpu.VMEM((8, count), I32),
             pltpu.VMEM((features, length + LANES), F32),
             pltpu.SemaphoreType.DMA,
             pltpu.SemaphoreType.DMA((streams,)),

time: 50.6 us -> 44.2 us (0.87)
  Pallas kernels: 20.5 us -> 14.1 us
    pallas_call x3, Pallas kernels: 6.29 us -> 3.26 us  [pack(): pl.pallas_call(body, in_specs=[IN_SMEM] + [IN_VMEM] * (3 + len(given)), o...]
    pallas_call x4, Pallas kernels: 6.38 us -> 3.87 us  [spread(): pl.pallas_call(body, in_specs=[IN_SMEM] + [IN_VMEM] * 3 + [IN_HBM] * len(...]
    pallas_call x1, Pallas kernels: 5.32 us -> 4.18 us  [pack_first(): pl.pallas_call(pack_first_body, in_specs=[IN_HBM, IN_HBM], out_specs=[IN_...]
  transfers between devices with their start and end apart: 11 -> 11, of which waited for: 6 -> 6; matrix products, arithmetic and copies ran while one was open for 0% -> 0% of each run, Pallas kernels for 25% -> 16%
where the time goes in v2:
time: 44.2 us; the launch traced here: 44.1 us
  starting transfers between devices  16.6 us (38%)
  Pallas kernels  14.1 us (32%)
  waiting for transfers between devices  12.6 us (29%)
  between operations  0.75 us (2%)
    ppermute x7, starting transfers between devices, exchanged(): lax.ppermute(totals, axis, [(k, k ^ 2 * bit - 1) for k in range(count)])  13.1 us
    ppermute x7, waiting for transfers between devices, exchanged(): lax.ppermute(totals, axis, [(k, k ^ 2 * bit - 1) for k in range(count)])  12.6 us
    pallas_call x1, Pallas kernels, pack_first(): pl.pallas_call(pack_first_body, in_specs=[IN_HBM, IN_HBM], out_specs=[IN_...  4.18 us
    pallas_call x4, Pallas kernels, spread(): pl.pallas_call(body, in_specs=[IN_SMEM] + [IN_VMEM] * 3 + [IN_HBM] * len(...  3.87 us
    ppermute x4, starting transfers between devices, from_behind(): lax.ppermute(value, ROWS, [(k, (k + 1) % count) for k in range(count)])  3.59 us
    pallas_call x3, Pallas kernels, pack(): pl.pallas_call(body, in_specs=[IN_SMEM] + [IN_VMEM] * (3 + len(given)), o...  3.26 us
    pallas_call x1, Pallas kernels, finish(): pl.pallas_call(body, in_specs=[IN_VMEM] * 2 + [IN_HBM] + [IN_VMEM] * (1 +...  2.73 us
  transfers between devices with their start and end apart: 11, of which 6 were waited for; matrix products, arithmetic and copies ran while one was open for 0% of the time, Pallas kernels for 16%

profile of v2, /device:TPU:0, one launch (start us, length us, event | category | flops | bytes accessed | tf_op | source)
XLA Modules:
  0.0 44.1 jit_solution(1950924714002815521)
XLA Ops:
  0.6 4.2 %pack_first.1 = (f32[4,32,16384]{2,1,0:T(8,128)S(1)}, f32[256,128]{1,0:T(8,128)S(1)}, s32[256,128]{1,0:T(8,128)S(1)}, s32[256,128]{1,0:T(8,128)S(1)}, s32[8,256]...) custom-call(s32[4,8192]{1,0:T(4,128)} %keep_hbm.1, f32[4,32,8192]{2,1,0:T(8,128)} %events.1), custom_call_target="tpu_custom_call" | custom-call | tf_op jit(solution)/shard_map/pack_first/pallas_call | solution.py:247
  4.8 0.1 collective-permute-start.3
  4.9 1.1 %pack.3 = (f32[4,32,16384]{2,1,0:T(8,128)S(1)}, f32[1,32,4096]{2,1,0:T(8,128)S(1)}) custom-call(s32[8,256]{1,0:T(8,128)S(4)} %get-tuple-element.21.starts, f32[256,128]{1,0:T(8,128)S(1)} %get-tuple-element.22.flat, f32[4,32,16384]{2,1,0:T(8,128)S(1)} %get-tuple-element.23._, s32[256,128]{1,0:T(8,128)S(1)} %get-tuple-element.24.index), custom_call_target="tpu_custom_call", output_to_operand_aliasing={{0}: (2, {})} | custom-call | tf_op jit(solution)/shard_map/pack/pallas_call | solution.py:276
  6.0 1.8 %collective-permute-start.2 = (f32[1,32,4096]{2,1,0:T(8,128)S(1)}, f32[1,32,4096]{2,1,0:T(8,128)S(1)}, u32[]{:S(2)}, u32[]{:S(2)}) collective-permute-start(f32[1,32,4096]{2,1,0:T(8,128)S(1)} %get-tuple-element.29), channel_id=1, source_target_pairs={{0,1},{1,2},{2,3},{3,4},{4,5},{5,6},{6,7},{7,8},{8,9},{9,10},{10,1... | collective-permute-start | bytes 1572872 | tf_op jit(solution)/shard_map/ppermute | solution.py:429
  7.8 1.1 %pack.4 = (f32[4,32,16384]{2,1,0:T(8,128)S(1)}, f32[1,32,4096]{2,1,0:T(8,128)S(1)}) custom-call(s32[8,256]{1,0:T(8,128)S(4)} %get-tuple-element.21.starts, f32[256,128]{1,0:T(8,128)S(1)} %get-tuple-element.22.flat, f32[4,32,16384]{2,1,0:T(8,128)S(1)} %get-tuple-element.25._, s32[256,128]{1,0:T(8,128)S(1)} %get-tuple-element.24.index), custom_call_target="tpu_custom_call", output_to_operand_aliasing={{0}: (2, {})} | custom-call | tf_op jit(solution)/shard_map/pack/pallas_call | solution.py:276
  8.9 0.1 collective-permute-start.1
  9.0 1.1 %pack.5 = (f32[4,32,16384]{2,1,0:T(8,128)S(1)}, f32[1,32,4096]{2,1,0:T(8,128)S(1)}) custom-call(s32[8,256]{1,0:T(8,128)S(4)} %get-tuple-element.21.starts, f32[256,128]{1,0:T(8,128)S(1)} %get-tuple-element.22.flat, f32[4,32,16384]{2,1,0:T(8,128)S(1)} %get-tuple-element.26._, s32[256,128]{1,0:T(8,128)S(1)} %get-tuple-element.24.index), custom_call_target="tpu_custom_call", output_to_operand_aliasing={{0}: (2, {})} | custom-call | tf_op jit(solution)/shard_map/pack/pallas_call | solution.py:276
  10.0 1.7 %collective-permute-start = (f32[1,32,4096]{2,1,0:T(8,128)S(1)}, f32[1,32,4096]{2,1,0:T(8,128)S(1)}, u32[]{:S(2)}, u32[]{:S(2)}) collective-permute-start(f32[1,32,4096]{2,1,0:T(8,128)S(1)} %get-tuple-element.27), channel_id=1, source_target_pairs={{0,1},{1,2},{2,3},{3,4},{4,5},{5,6},{6,7},{7,8},{8,9},{9,10},{10,1... | collective-permute-start | bytes 1572872 | tf_op jit(solution)/shard_map/ppermute | solution.py:429
  11.7 0.1 collective-permute-start.4
  11.8 1.4 %collective-permute-done.4.refs_0_ = f32[8,128]{1,0:T(8,128)S(1)} collective-permute-done((f32[8,128]{1,0:T(8,128)S(1)}, f32[8,128]{1,0:T(8,128)S(1)}, u32[]{:S(2)}, u32[]{:S(2)}) %collective-permute-start.4) | collective-permute-done | bytes 4128 | tf_op jit(solution)/shard_map/ppermute | solution.py:420
  13.2 1.6 %collective-permute-start.5 = (f32[8,128]{1,0:T(8,128)S(1)}, f32[8,128]{1,0:T(8,128)S(1)}, u32[]{:S(2)}, u32[]{:S(2)}) collective-permute-start(f32[8,128]{1,0:T(8,128)S(1)} %add.15.chip), channel_id=1, source_target_pairs={{0,8},{8,0},{16,24},{24,16},{1,9},{9,1},{17,25},{25,17},{2,10},{10... | collective-permute-start | bytes 12296 | tf_op jit(solution)/shard_map/ppermute | solution.py:420
  14.8 2.0 %collective-permute-done.5.refs_2_ = f32[8,128]{1,0:T(8,128)S(1)} collective-permute-done((f32[8,128]{1,0:T(8,128)S(1)}, f32[8,128]{1,0:T(8,128)S(1)}, u32[]{:S(2)}, u32[]{:S(2)}) %collective-permute-start.5) | collective-permute-done | bytes 4128 | tf_op jit(solution)/shard_map/ppermute | solution.py:420
  16.9 3.4 %collective-permute-start.6 = (f32[8,128]{1,0:T(8,128)S(1)}, f32[8,128]{1,0:T(8,128)S(1)}, u32[]{:S(2)}, u32[]{:S(2)}) collective-permute-start(f32[8,128]{1,0:T(8,128)S(1)} %add.16), channel_id=1, source_target_pairs={{0,24},{8,16},{16,8},{24,0},{1,25},{9,17},{17,9},{25,1},{2,26},{10... | collective-permute-start | bytes 12296 | tf_op jit(solution)/shard_map/ppermute | solution.py:420
  20.2 1.9 %collective-permute-done.6.refs_3_ = f32[8,128]{1,0:T(8,128)S(1)} collective-permute-done((f32[8,128]{1,0:T(8,128)S(1)}, f32[8,128]{1,0:T(8,128)S(1)}, u32[]{:S(2)}, u32[]{:S(2)}) %collective-permute-start.6) | collective-permute-done | bytes 4128 | tf_op jit(solution)/shard_map/ppermute | solution.py:420
  22.2 1.9 %collective-permute-start.7 = (f32[8,128]{1,0:T(8,128)S(1)}, f32[8,128]{1,0:T(8,128)S(1)}, u32[]{:S(2)}, u32[]{:S(2)}) collective-permute-start(f32[8,128]{1,0:T(8,128)S(1)} %add.17), channel_id=1, source_target_pairs={{0,32},{32,0},{64,96},{96,64},{1,33},{33,1},{65,97},{97,65},{2,34}... | collective-permute-start | bytes 12296 | tf_op jit(solution)/shard_map/ppermute | solution.py:420
  24.1 1.7 %collective-permute-done.7.refs_0_ = f32[8,128]{1,0:T(8,128)S(1)} collective-permute-done((f32[8,128]{1,0:T(8,128)S(1)}, f32[8,128]{1,0:T(8,128)S(1)}, u32[]{:S(2)}, u32[]{:S(2)}) %collective-permute-start.7) | collective-permute-done | bytes 4128 | tf_op jit(solution)/shard_map/ppermute | solution.py:420
  25.8 4.4 %collective-permute-start.8 = (f32[8,128]{1,0:T(8,128)S(1)}, f32[8,128]{1,0:T(8,128)S(1)}, u32[]{:S(2)}, u32[]{:S(2)}) collective-permute-start(f32[8,128]{1,0:T(8,128)S(1)} %add.18), channel_id=1, source_target_pairs={{0,96},{32,64},{64,32},{96,0},{1,97},{33,65},{65,33},{97,1},{2,98}... | collective-permute-start | bytes 12296 | tf_op jit(solution)/shard_map/ppermute | solution.py:420
  30.1 1.9 %collective-permute-done.8.refs_1_ = f32[8,128]{1,0:T(8,128)S(1)} collective-permute-done((f32[8,128]{1,0:T(8,128)S(1)}, f32[8,128]{1,0:T(8,128)S(1)}, u32[]{:S(2)}, u32[]{:S(2)}) %collective-permute-start.8) | collective-permute-done | bytes 4128 | tf_op jit(solution)/shard_map/ppermute | solution.py:420
  32.1 0.1 collective-permute-start.9
  32.2 3.6 %collective-permute-done.9.refs_1_ = f32[8,128]{1,0:T(8,128)S(1)} collective-permute-done((f32[8,128]{1,0:T(8,128)S(1)}, f32[8,128]{1,0:T(8,128)S(1)}, u32[]{:S(2)}, u32[]{:S(2)}) %collective-permute-start.9) | collective-permute-done | bytes 4128 | tf_op jit(solution)/shard_map/ppermute | solution.py:420
  35.8 1.6 %collective-permute-start.10 = (f32[8,128]{1,0:T(8,128)S(1)}, f32[8,128]{1,0:T(8,128)S(1)}, u32[]{:S(2)}, u32[]{:S(2)}) collective-permute-start(f32[8,128]{1,0:T(8,128)S(1)} %add.19), channel_id=1, source_target_pairs={{0,6},{2,4},{4,2},{6,0},{1,7},{3,5},{5,3},{7,1},{8,14},{10,12},{12... | collective-permute-start | bytes 12296 | tf_op jit(solution)/shard_map/ppermute | solution.py:420
  37.4 0.0 collective-permute-done.3.arrived
  37.4 0.7 %spread.4._ = f32[4,32,16384]{2,1,0:T(8,128)S(1)} custom-call(s32[8,256]{1,0:T(8,128)S(4)} %get-tuple-element.21.starts, f32[1,32,4096]{2,1,0:T(8,128)S(1)} %collective-permute-done.3.arrived, f32[4,32,16384]{2,1,0:T(8,128)S(1)} %get-tuple-element.31._, s32[256,128]{1,0:T(8,128)S(1)} %get-tuple-element.32.ranks), custom_call_target="tpu_custom_call", output_to_operand_aliasing={{}: (2, {})} | custom-call | tf_op jit(solution)/shard_map/spread/pallas_call | solution.py:309
  38.0 0.0 collective-permute-done.2.arrived
  38.1 1.1 %spread.5 = (f32[4,32,16384]{2,1,0:T(8,128)S(1)}, f32[4,32,8192]{2,1,0:T(8,128)}) custom-call(s32[8,256]{1,0:T(8,128)S(4)} %get-tuple-element.21.starts, f32[1,32,4096]{2,1,0:T(8,128)S(1)} %collective-permute-done.2.arrived, f32[4,32,16384]{2,1,0:T(8,128)S(1)} %spread.4._, s32[256,128]{1,0:T(8,128)S(1)} %get-tuple-element.32.ranks), custom_call_target="tpu_custom_call", output_to_operand_aliasing={{0}: (2, {})} | custom-call | tf_op jit(solution)/shard_map/spread/pallas_call | solution.py:309
  39.1 0.0 collective-permute-done.1.arrived
  39.1 1.1 %spread.6 = (f32[4,32,16384]{2,1,0:T(8,128)S(1)}, f32[4,32,8192]{2,1,0:T(8,128)}) custom-call(s32[8,256]{1,0:T(8,128)S(4)} %get-tuple-element.21.starts, f32[1,32,4096]{2,1,0:T(8,128)S(1)} %collective-permute-done.1.arrived, f32[4,32,16384]{2,1,0:T(8,128)S(1)} %get-tuple-element.33._, ...), custom_call_target="tpu_custom_call", output_to_operand_aliasing={{0}: (2, {}), {1}: (4, {})} | custom-call | tf_op jit(solution)/shard_map/spread/pallas_call | solution.py:309
  40.2 0.0 collective-permute-done.arrived
  40.2 1.1 %spread.7 = (f32[4,32,16384]{2,1,0:T(8,128)S(1)}, f32[4,32,8192]{2,1,0:T(8,128)}) custom-call(s32[8,256]{1,0:T(8,128)S(4)} %get-tuple-element.21.starts, f32[1,32,4096]{2,1,0:T(8,128)S(1)} %collective-permute-done.arrived, f32[4,32,16384]{2,1,0:T(8,128)S(1)} %get-tuple-element.35._, ...), custom_call_target="tpu_custom_call", output_to_operand_aliasing={{0}: (2, {}), {1}: (4, {})} | custom-call | tf_op jit(solution)/shard_map/spread/pallas_call | solution.py:309
  41.3 0.0 collective-permute-done.10.refs_2_
  41.3 2.7 %finish.1 = (f32[4,32,8192]{2,1,0:T(8,128)}, f32[4,32,8192]{2,1,0:T(8,128)}) custom-call(f32[4,32,16384]{2,1,0:T(8,128)S(1)} %get-tuple-element.37.state, s32[256,128]{1,0:T(8,128)S(1)} %get-tuple-element.32.ranks, f32[4,32,8192]{2,1,0:T(8,128)} %get-tuple-element.38._, f32[8,128]{1,0:T(8,128)S(1)} %between.1.own, ...), custom_call_target="tpu_custom_call", output_to_operand_aliasing={{0}: (2, {})} | custom-call | tf_op jit(solution)/shard_map/finish/pallas_call | solution.py:397
  (6 shorter events, 0.0 us)
Async XLA Ops:
  4.8 32.6 %collective-permute-start.3 = (f32[1,32,4096]{2,1,0:T(8,128)S(1)}, f32[1,32,4096]{2,1,0:T(8,128)S(1)}, u32[]{:S(2)}, u32[]{:S(2)}) collective-permute-start(f32[1,32,4096]{2,1,0:T(8,128)S(1)} %get-tuple-element.30), channel_id=1, source_target_pairs={{0,1},{1,2},{2,3},{3,4},{4,5},{5,6},{6,7},{7,8},{8,9},{9,10},{10,1... | collective-permute-start | bytes 1572872 | tf_op jit(solution)/shard_map/ppermute | solution.py:429
  6.0 32.1 %collective-permute-start.2 = (f32[1,32,4096]{2,1,0:T(8,128)S(1)}, f32[1,32,4096]{2,1,0:T(8,128)S(1)}, u32[]{:S(2)}, u32[]{:S(2)}) collective-permute-start(f32[1,32,4096]{2,1,0:T(8,128)S(1)} %get-tuple-element.29), channel_id=1, source_target_pairs={{0,1},{1,2},{2,3},{3,4},{4,5},{5,6},{6,7},{7,8},{8,9},{9,10},{10,1... | collective-permute-start | bytes 1572872 | tf_op jit(solution)/shard_map/ppermute | solution.py:429
  8.9 30.3 %collective-permute-start.1 = (f32[1,32,4096]{2,1,0:T(8,128)S(1)}, f32[1,32,4096]{2,1,0:T(8,128)S(1)}, u32[]{:S(2)}, u32[]{:S(2)}) collective-permute-start(f32[1,32,4096]{2,1,0:T(8,128)S(1)} %get-tuple-element.28), channel_id=1, source_target_pairs={{0,1},{1,2},{2,3},{3,4},{4,5},{5,6},{6,7},{7,8},{8,9},{9,10},{10,1... | collective-permute-start | bytes 1572872 | tf_op jit(solution)/shard_map/ppermute | solution.py:429
  10.0 30.2 %collective-permute-start = (f32[1,32,4096]{2,1,0:T(8,128)S(1)}, f32[1,32,4096]{2,1,0:T(8,128)S(1)}, u32[]{:S(2)}, u32[]{:S(2)}) collective-permute-start(f32[1,32,4096]{2,1,0:T(8,128)S(1)} %get-tuple-element.27), channel_id=1, source_target_pairs={{0,1},{1,2},{2,3},{3,4},{4,5},{5,6},{6,7},{7,8},{8,9},{9,10},{10,1... | collective-permute-start | bytes 1572872 | tf_op jit(solution)/shard_map/ppermute | solution.py:429
  11.7 1.5 %collective-permute-start.4 = (f32[8,128]{1,0:T(8,128)S(1)}, f32[8,128]{1,0:T(8,128)S(1)}, u32[]{:S(2)}, u32[]{:S(2)}) collective-permute-start(f32[8,128]{1,0:T(8,128)S(1)} %get-tuple-element.39), channel_id=1, source_target_pairs={{0,1},{1,0},{2,3},{3,2},{4,5},{5,4},{6,7},{7,6},{8,9},{9,8},{10,11... | collective-permute-start | bytes 12296 | tf_op jit(solution)/shard_map/ppermute | solution.py:420
  13.2 3.6 %collective-permute-start.5 = (f32[8,128]{1,0:T(8,128)S(1)}, f32[8,128]{1,0:T(8,128)S(1)}, u32[]{:S(2)}, u32[]{:S(2)}) collective-permute-start(f32[8,128]{1,0:T(8,128)S(1)} %add.15.chip), channel_id=1, source_target_pairs={{0,8},{8,0},{16,24},{24,16},{1,9},{9,1},{17,25},{25,17},{2,10},{10... | collective-permute-start | bytes 12296 | tf_op jit(solution)/shard_map/ppermute | solution.py:420
  16.9 5.3 %collective-permute-start.6 = (f32[8,128]{1,0:T(8,128)S(1)}, f32[8,128]{1,0:T(8,128)S(1)}, u32[]{:S(2)}, u32[]{:S(2)}) collective-permute-start(f32[8,128]{1,0:T(8,128)S(1)} %add.16), channel_id=1, source_target_pairs={{0,24},{8,16},{16,8},{24,0},{1,25},{9,17},{17,9},{25,1},{2,26},{10... | collective-permute-start | bytes 12296 | tf_op jit(solution)/shard_map/ppermute | solution.py:420
  22.2 3.6 %collective-permute-start.7 = (f32[8,128]{1,0:T(8,128)S(1)}, f32[8,128]{1,0:T(8,128)S(1)}, u32[]{:S(2)}, u32[]{:S(2)}) collective-permute-start(f32[8,128]{1,0:T(8,128)S(1)} %add.17), channel_id=1, source_target_pairs={{0,32},{32,0},{64,96},{96,64},{1,33},{33,1},{65,97},{97,65},{2,34}... | collective-permute-start | bytes 12296 | tf_op jit(solution)/shard_map/ppermute | solution.py:420
  25.8 6.3 %collective-permute-start.8 = (f32[8,128]{1,0:T(8,128)S(1)}, f32[8,128]{1,0:T(8,128)S(1)}, u32[]{:S(2)}, u32[]{:S(2)}) collective-permute-start(f32[8,128]{1,0:T(8,128)S(1)} %add.18), channel_id=1, source_target_pairs={{0,96},{32,64},{64,32},{96,0},{1,97},{33,65},{65,33},{97,1},{2,98}... | collective-permute-start | bytes 12296 | tf_op jit(solution)/shard_map/ppermute | solution.py:420
  32.1 3.7 %collective-permute-start.9 = (f32[8,128]{1,0:T(8,128)S(1)}, f32[8,128]{1,0:T(8,128)S(1)}, u32[]{:S(2)}, u32[]{:S(2)}) collective-permute-start(f32[8,128]{1,0:T(8,128)S(1)} %between.1.own), channel_id=1, source_target_pairs={{0,2},{2,0},{4,6},{6,4},{1,3},{3,1},{5,7},{7,5},{8,10},{10,8},{12,... | collective-permute-start | bytes 12296 | tf_op jit(solution)/shard_map/ppermute | solution.py:420
  35.8 5.6 %collective-permute-start.10 = (f32[8,128]{1,0:T(8,128)S(1)}, f32[8,128]{1,0:T(8,128)S(1)}, u32[]{:S(2)}, u32[]{:S(2)}) collective-permute-start(f32[8,128]{1,0:T(8,128)S(1)} %add.19), channel_id=1, source_target_pairs={{0,6},{2,4},{4,2},{6,0},{1,7},{3,5},{5,3},{7,1},{8,14},{10,12},{12... | collective-permute-start | bytes 12296 | tf_op jit(solution)/shard_map/ppermute | solution.py:420

commit v3 on v2

--- a/solution.py
+++ b/solution.py
@@ -1,3 +1,5 @@
+import itertools
+
 import jax
 import jax.numpy as jnp
 from jax import lax
@@ -11,6 +13,7 @@
 LANES = 128
 GROUP = 64
 GROUP_SUM = 16
+PARTS = 2
 ROWS = ("rows_0", "rows_1", "rows_2", "rows_3")
 SHAPE = (4, 4, 4, 2)
 F32 = jnp.float32
@@ -134,7 +137,6 @@
     keep, scalars, work, copied, loaded,
 ):
     streams, length = keep.shape
-    features = events.shape[1]
     tiles = length // LANES
     loads = [
         pltpu.make_async_copy(events.at[s], state.at[s, :, pl.ds(0, length)], loaded.at[s])
@@ -156,59 +158,33 @@
     for load in loads[1:]:
         load.wait()
 
-    def step(g, sums):
-        sums = list(sums)
-        for j in range(GROUP_SUM):
-            t = g * GROUP_SUM + j
-            at = pl.multiple_of(t * LANES, LANES)
-            for s in range(1, streams):
-                kept = state[s, :, pl.ds(at, LANES)] * flat[pl.ds(t * streams + s, 1), :]
-                sums[s - 1] = sums[s - 1] + kept
-        return tuple(sums)
-
-    zero = jnp.zeros((features, LANES), F32)
-    sums = lax.fori_loop(0, tiles // GROUP_SUM, step, (zero,) * (streams - 1))
     sublane = lax.broadcasted_iota(I32, (8, LANES), 0)
     lane = lanes_of(8)
     counts = jnp.zeros((8, LANES), F32)
     for s in range(streams):
         counts = jnp.where(lane == s, starts[2, (tiles - 1) * streams + s].astype(F32), counts)
-    line = totals_line(0, total)
-    for s in range(1, streams):
-        whole_sum = jnp.broadcast_to(
-            jnp.sum(sums[s - 1], axis=1, keepdims=True), (features, LANES)
-        )
-        line = line + totals_line(s, whole_sum)
-    line = jnp.broadcast_to(line, (8, LANES))
+    line = jnp.broadcast_to(totals_line(0, total), (8, LANES))
     totals[...] = jnp.where(sublane == 0, line, jnp.where(sublane == 1, counts, 0.0))
 
 
-def spread_stream(s, at_stream, streams, length, starts, arrived, state, ranks, joint):
+def joined(s, length, arrived, state, joint):
+    joint[:, :SPAN] = jnp.where(lax.axis_index(ROWS) > 0, arrived[0], 0.0)
+    joint[:, SPAN:] = state[s, :, length : length + SPAN + LANES]
+
+
+def window_mean(s, t, streams, starts, state, ranks, joint):
     features = state.shape[1]
-    lane = lanes_of(features)
-    joint[:, :SPAN] = jnp.where(lax.axis_index(ROWS) > 0, arrived[at_stream], 0.0)
-    joint[:, SPAN:] = state[s, :, length : length + SPAN + LANES]
-
-    def step(g, carry):
-        for j in range(GROUP):
-            t = g * GROUP + j
-            row = t * streams + s
-            at = pl.multiple_of(t * LANES, LANES)
-            base = starts[1, row]
-            low_at = pl.multiple_of((base >> 7) * LANES, LANES)
-            window = jnp.where(
-                lane >= (base & (LANES - 1)),
-                joint[:, pl.ds(low_at, LANES)],
-                joint[:, pl.ds(low_at + LANES, LANES)],
-            )
-            order = jnp.broadcast_to(ranks[pl.ds(row, 1), :] & (LANES - 1), (features, LANES))
-            running = state[s, :, pl.ds(at, LANES)]
-            state[s, :, pl.ds(length + at, LANES)] = (
-                running - picked_lanes(window, order)
-            ) * (1.0 / SPAN)
-        return carry
-
-    lax.fori_loop(0, length // LANES // GROUP, step, 0)
+    row = t * streams + s
+    base = starts[1, row]
+    low_at = pl.multiple_of((base >> 7) * LANES, LANES)
+    window = jnp.where(
+        lanes_of(features) >= (base & (LANES - 1)),
+        joint[:, pl.ds(low_at, LANES)],
+        joint[:, pl.ds(low_at + LANES, LANES)],
+    )
+    order = jnp.broadcast_to(ranks[row : row + 1, :] & (LANES - 1), (features, LANES))
+    running = state[s, :, t * LANES : (t + 1) * LANES]
+    return running, (running - picked_lanes(window, order)) * (1.0 / SPAN)
 
 
 def means_of(s, length, state):
@@ -288,7 +264,45 @@
     )(starts, flat, state, index, *given)
 
 
-def spread(s, at_stream, length, starts, arrived, state, ranks, lagging):
+def add_totals(length, flat, state, totals):
+    streams, features, _ = state.shape
+    tiles = length // LANES
+
+    def body(flat, _, so_far, state, totals):
+        def step(g, sums):
+            sums = list(sums)
+            for j in range(GROUP_SUM):
+                t = g * GROUP_SUM + j
+                at = pl.multiple_of(t * LANES, LANES)
+                for s in range(1, streams):
+                    kept = state[s, :, pl.ds(at, LANES)] * flat[pl.ds(t * streams + s, 1), :]
+                    sums[s - 1] = sums[s - 1] + kept
+            return tuple(sums)
+
+        zero = jnp.zeros((features, LANES), F32)
+        sums = lax.fori_loop(0, tiles // GROUP_SUM, step, (zero,) * (streams - 1))
+        line = jnp.zeros((1, LANES), F32)
+        for s in range(1, streams):
+            whole_sum = jnp.broadcast_to(
+                jnp.sum(sums[s - 1], axis=1, keepdims=True), (features, LANES)
+            )
+            line = line + totals_line(s, whole_sum)
+        sublane = lax.broadcasted_iota(I32, (8, LANES), 0)
+        line = jnp.broadcast_to(line, (8, LANES))
+        totals[...] = so_far[...] + jnp.where(sublane == 0, line, 0.0)
+
+    return pl.pallas_call(
+        body,
+        in_specs=[IN_VMEM] * 3,
+        out_specs=[IN_VMEM] * 2,
+        out_shape=[pltpu.VMEM(state.shape, F32), pltpu.VMEM((8, LANES), F32)],
+        input_output_aliases={1: 0},
+        compiler_params=PARAMS,
+        name="add_totals",
+    )(flat, state, totals)
+
+
+def spread(s, length, starts, arrived, state, ranks, lagging):
     streams, features, _ = state.shape
 
     def body(starts, arrived, _, ranks, *refs):
@@ -298,7 +312,10 @@
         if s:
             write = pltpu.make_async_copy(means_of(s - 1, length, state), outs[-1].at[s - 1], sent)
             write.start()
-        spread_stream(s, at_stream, streams, length, starts, arrived, state, ranks, joint)
+        joined(s, length, arrived, state, joint)
+        for t in range(length // LANES):
+            _, mean = window_mean(s, t, streams, starts, state, ranks, joint)
+            state[s, :, length + t * LANES : length + (t + 1) * LANES] = mean
         if write is not None:
             write.wait()
 
@@ -344,7 +361,7 @@
     )(chip, *parts)
 
 
-def finish(length, state, ranks, lagging, own, core, rows):
+def deviate(length, state, ranks, lagging, own, core, rows, sides):
     streams, features, _ = state.shape
     last = streams - 1
     tiles = length // LANES
@@ -352,9 +369,14 @@
 
     def body(state, ranks, _, own, *refs):
         core_parts, row_parts = (refs[: len(core)], refs[len(core) : len(refs) - 7])
+        at_core = lax.axis_index(ROWS[3])
+        row_parts = [
+            jnp.where(at_core == sides[k], row_parts[2 * k][0:4, :], row_parts[2 * k + 1][0:4, :])
+            for k in range(len(sides))
+        ]
         lagging, deviation, columns, scale, staged, sent, gone = refs[-7:]
         writes = [
-            pltpu.make_async_copy(means_of(last, length, state), lagging.at[last], sent)
+            pltpu.make_async_copy(means_of(last - 1, length, state), lagging.at[last - 1], sent)
         ]
         writes[0].start()
         before = own[2:4, :] + earlier_rows(core_parts, ROWS[3]) + earlier_rows(row_parts, ROWS[2])
@@ -373,20 +395,14 @@
             tally = jnp.sum(jnp.where(lanes_of(1) == s, before[1:2, :], 0.0))
             seen = jnp.where(stream == s, tally, seen)
         scale[...] = 1.0 / jnp.maximum(seen + ranks[...].astype(F32), 1.0)
-        for s in range(streams):
+        for s in range(last):
             column = columns[s]
-
-            def step(g, carry, s=s, column=column):
-                for j in range(GROUP):
-                    t = g * GROUP + j
-                    at = pl.multiple_of(t * LANES, LANES)
-                    running = state[s, :, pl.ds(at, LANES)]
-                    staged[s, :, pl.ds(at, LANES)] = state[s, :, pl.ds(length + at, LANES)] - (
-                        column + running
-                    ) * scale[pl.ds(t * streams + s, 1), :]
-                return carry
-
-            lax.fori_loop(0, tiles // GROUP, step, 0)
+            for t in range(tiles):
+                at = slice(t * LANES, (t + 1) * LANES)
+                mean = state[s, :, length + t * LANES : length + (t + 1) * LANES]
+                staged[s, :, at] = mean - (column + state[s, :, at]) * scale[
+                    t * streams + s : t * streams + s + 1, :
+                ]
             write = pltpu.make_async_copy(staged.at[s], deviation.at[s], gone.at[s])
             write.start()
             writes.append(write)
@@ -397,19 +413,75 @@
     return pl.pallas_call(
         body,
         in_specs=[IN_VMEM] * 2 + [IN_HBM] + [IN_VMEM] * (1 + len(core) + len(rows)),
-        out_specs=[IN_HBM, IN_HBM],
-        out_shape=[shape, shape],
-        scratch_shapes=[
+        out_specs=[IN_HBM, IN_HBM, IN_VMEM, IN_VMEM],
+        out_shape=[
+            shape,
+            shape,
             pltpu.VMEM((streams, features, LANES), F32),
             pltpu.VMEM((count, LANES), F32),
-            pltpu.VMEM((streams, features, length), F32),
+        ],
+        scratch_shapes=[
+            pltpu.VMEM((last, features, length), F32),
             pltpu.SemaphoreType.DMA,
-            pltpu.SemaphoreType.DMA((streams,)),
+            pltpu.SemaphoreType.DMA((last,)),
         ],
         input_output_aliases={2: 0},
         compiler_params=PARAMS,
+        name="deviate",
+    )(state, ranks, lagging, own, *core, *rows)
+
+
+def finish(length, starts, arrived, state, ranks, columns, scale, outputs):
+    streams, features, _ = state.shape
+    s = streams - 1
+    tiles = length // LANES
+
+    def body(starts, arrived, state, ranks, columns, scale, *refs):
+        lagging, deviation, joint, means, deviations, sent, gone = refs[-7:]
+        joined(s, length, arrived, state, joint)
+        column = columns[s]
+        writes = []
+        for part in range(PARTS):
+            for t in range(part * tiles // PARTS, (part + 1) * tiles // PARTS):
+                at = slice(t * LANES, (t + 1) * LANES)
+                running, mean = window_mean(s, t, streams, starts, state, ranks, joint)
+                means[:, at] = mean
+                deviations[:, at] = mean - (column + running) * scale[
+                    t * streams + s : t * streams + s + 1, :
+                ]
+            at = pl.ds(part * length // PARTS, length // PARTS)
+            for source, target, done in ((means, lagging, sent), (deviations, deviation, gone)):
+                writes.append(
+                    pltpu.make_async_copy(source.at[:, at], target.at[s, :, at], done.at[part])
+                )
+                writes[-1].start()
+        for write in writes:
+            write.wait()
+
+    return pl.pallas_call(
+        body,
+        in_specs=[IN_SMEM] + [IN_VMEM] * 5 + [IN_HBM] * 2,
+        out_specs=[IN_HBM] * 2,
+        out_shape=[jax.ShapeDtypeStruct((streams, features, length), F32)] * 2,
+        scratch_shapes=[
+            pltpu.VMEM((features, 2 * SPAN + LANES), F32),
+            pltpu.VMEM((features, length), F32),
+            pltpu.VMEM((features, length), F32),
+            pltpu.SemaphoreType.DMA((PARTS,)),
+            pltpu.SemaphoreType.DMA((PARTS,)),
+        ],
+        input_output_aliases={6: 0, 7: 1},
+        compiler_params=PARAMS,
         name="finish",
-    )(state, ranks, lagging, own, *core, *rows)
+    )(starts, arrived, state, ranks, columns, scale, *outputs)
+
+
+def permuted(value, target):
+    places = list(itertools.product(*(range(lax.axis_size(axis)) for axis in ROWS)))
+    number = {place: k for k, place in enumerate(places)}
+    return lax.ppermute(
+        value, ROWS, [(number[place], number[target(*place)]) for place in places]
+    )
 
 
 def exchanged(totals, axis):
@@ -417,13 +489,40 @@
     brought = []
     bit = 1
     while bit < count:
-        other = lax.ppermute(totals, axis, [(k, k ^ (2 * bit - 1)) for k in range(count)])
+        flip = 2 * bit - 1
+
+        def target(z, y, x, core, flip=flip):
+            return (z ^ flip, y, x, 1 - core) if axis == ROWS[0] else (z, y ^ flip, x, 1 - core)
+
+        other = permuted(totals, target)
         brought.append(other)
         totals = totals + other
         bit *= 2
     return brought, totals
 
 
+def other_core(value):
+    return permuted(value, lambda z, y, x, core: (z, y, x, 1 - core))
+
+
+def exchanged_rows(totals):
+    count = lax.axis_size(ROWS[2])
+    brought, sides = ([], [])
+    bit = 1
+    while bit < count:
+        flip, side = (2 * bit - 1, int(2 * bit >= count))
+
+        def target(z, y, x, core, flip=flip, side=side):
+            return (z, y, (x - 1) % count, 1 - side) if core else (z, y, x ^ flip, side)
+
+        other = permuted(totals, target)
+        brought += [other, other_core(other)]
+        sides.append(side)
+        totals = totals + other
+        bit *= 2
+    return brought, sides
+
+
 def from_behind(value):
     count = lax.axis_size(ROWS)
     return lax.ppermute(value, ROWS, [(k, (k + 1) % count) for k in range(count)])
@@ -433,21 +532,24 @@
     streams, _, length = events.shape
     state, flat, index, ranks, starts, tail, totals = pack_first(keep, events)
     arrived = [from_behind(tail)]
+    state, totals = add_totals(length, flat, state, totals)
     for s in range(1, streams):
         state, tail = pack(s, length, starts, flat, state, index, 0, 1)
         arrived.append(from_behind(tail))
-    brought = {}
-    for axis in (ROWS[3], ROWS[1], ROWS[0]):
+    brought = {ROWS[3]: [other_core(totals)]}
+    chip = totals = totals + brought[ROWS[3]][0]
+    for axis in (ROWS[1], ROWS[0]):
         brought[axis], totals = exchanged(totals, axis)
-        if axis == ROWS[3]:
-            chip = totals
     own = between(chip, brought)
-    rows, _ = exchanged(own, ROWS[2])
+    rows, sides = exchanged_rows(own)
     lagging = None
-    for s in range(streams):
-        state, lagging = spread(s, 0, length, starts, arrived[s], state, ranks, lagging)
+    for s in range(streams - 1):
+        state, lagging = spread(s, length, starts, arrived[s], state, ranks, lagging)
+    *outputs, columns, scale = deviate(
+        length, state, ranks, lagging, own, brought[ROWS[3]], rows, sides
+    )
     return tuple(
-        finish(length, state, ranks, lagging, own, brought[ROWS[3]], rows)
+        finish(length, starts, arrived[-1], state, ranks, columns, scale, outputs)
     )
 
 

time: 44.2 us -> 47.4 us (1.072)
  the two profiles are of different devices: /device:TPU:0 before, /device:TPU:1 now
where the time goes in v3:
time: 47.4 us; the launch traced here: 47.3 us
  starting transfers between devices  16.9 us (36%)
  waiting for transfers between devices  15.2 us (32%)
  Pallas kernels  14.2 us (30%)
  between operations  0.92 us (2%)
    ppermute x9, waiting for transfers between devices, permuted(): lax.ppermute(value, ROWS, [(number[place], number[target(*place)]) for pl...  15.2 us
    ppermute x9, starting transfers between devices, permuted(): lax.ppermute(value, ROWS, [(number[place], number[target(*place)]) for pl...  12.5 us
    ppermute x4, starting transfers between devices, from_behind(): lax.ppermute(value, ROWS, [(k, (k + 1) % count) for k in range(count)])  4.49 us
    pallas_call x1, Pallas kernels, pack_first(): pl.pallas_call(pack_first_body, in_specs=[IN_HBM, IN_HBM], out_specs=[IN_...  3.65 us
    pallas_call x3, Pallas kernels, pack(): pl.pallas_call(body, in_specs=[IN_SMEM] + [IN_VMEM] * (3 + len(given)), o...  3.26 us
    pallas_call x3, Pallas kernels, spread(): pl.pallas_call(body, in_specs=[IN_SMEM] + [IN_VMEM] * 3 + [IN_HBM] * len(...  2.8 us
    pallas_call x1, Pallas kernels, deviate(): pl.pallas_call(body, in_specs=[IN_VMEM] * 2 + [IN_HBM] + [IN_VMEM] * (1 +...  2.2 us
    pallas_call x1, Pallas kernels, finish(): pl.pallas_call(body, in_specs=[IN_SMEM] + [IN_VMEM] * 5 + [IN_HBM] * 2, o...  1.76 us
  transfers between devices with their start and end apart: 13, of which 7 were waited for; matrix products, arithmetic and copies ran while one was open for 0% of the time, Pallas kernels for 19%

profile of v3, /device:TPU:1, one launch (start us, length us, event | category | flops | bytes accessed | tf_op | source)
XLA Modules:
  0.0 47.3 jit_solution(2523120044612608586)
XLA Ops:
  0.6 3.6 %pack_first.1 = (f32[4,32,16384]{2,1,0:T(8,128)S(1)}, f32[256,128]{1,0:T(8,128)S(1)}, s32[256,128]{1,0:T(8,128)S(1)}, s32[256,128]{1,0:T(8,128)S(1)}, s32[8,256]...) custom-call(s32[4,8192]{1,0:T(4,128)} %keep_hbm.1, f32[4,32,8192]{2,1,0:T(8,128)} %events.1), custom_call_target="tpu_custom_call" | custom-call | tf_op jit(solution)/shard_map/pack_first/pallas_call | solution.py:223
  4.3 2.7 %collective-permute-start.3 = (f32[1,32,4096]{2,1,0:T(8,128)S(1)}, f32[1,32,4096]{2,1,0:T(8,128)S(1)}, u32[]{:S(2)}, u32[]{:S(2)}) collective-permute-start(f32[1,32,4096]{2,1,0:T(8,128)S(1)} %get-tuple-element.36), channel_id=1, source_target_pairs={{0,1},{1,2},{2,3},{3,4},{4,5},{5,6},{6,7},{7,8},{8,9},{9,10},{10,1... | collective-permute-start | bytes 1572872 | tf_op jit(solution)/shard_map/ppermute | solution.py:528
  6.9 0.5 %add_totals.1 = (f32[4,32,16384]{2,1,0:T(8,128)S(1)}, f32[8,128]{1,0:T(8,128)S(1)}) custom-call(f32[256,128]{1,0:T(8,128)S(1)} %get-tuple-element.26.flat, f32[4,32,16384]{2,1,0:T(8,128)S(1)} %get-tuple-element.27._, f32[8,128]{1,0:T(8,128)S(1)} %get-tuple-element.28.so_far), custom_call_target="tpu_custom_call", output_to_operand_aliasing={{0}: (1, {})} | custom-call | tf_op jit(solution)/shard_map/add_totals/pallas_call | solution.py:294
  7.5 1.1 %pack.3 = (f32[4,32,16384]{2,1,0:T(8,128)S(1)}, f32[1,32,4096]{2,1,0:T(8,128)S(1)}) custom-call(s32[8,256]{1,0:T(8,128)S(4)} %get-tuple-element.25.starts, f32[256,128]{1,0:T(8,128)S(1)} %get-tuple-element.26.flat, f32[4,32,16384]{2,1,0:T(8,128)S(1)} %get-tuple-element.29._, s32[256,128]{1,0:T(8,128)S(1)} %get-tuple-element.30.index), custom_call_target="tpu_custom_call", output_to_operand_aliasing={{0}: (2, {})} | custom-call | tf_op jit(solution)/shard_map/pack/pallas_call | solution.py:252
  8.6 0.1 collective-permute-start.2
  8.7 1.1 %pack.4 = (f32[4,32,16384]{2,1,0:T(8,128)S(1)}, f32[1,32,4096]{2,1,0:T(8,128)S(1)}) custom-call(s32[8,256]{1,0:T(8,128)S(4)} %get-tuple-element.25.starts, f32[256,128]{1,0:T(8,128)S(1)} %get-tuple-element.26.flat, f32[4,32,16384]{2,1,0:T(8,128)S(1)} %get-tuple-element.31._, s32[256,128]{1,0:T(8,128)S(1)} %get-tuple-element.30.index), custom_call_target="tpu_custom_call", output_to_operand_aliasing={{0}: (2, {})} | custom-call | tf_op jit(solution)/shard_map/pack/pallas_call | solution.py:252
  9.8 1.7 %collective-permute-start.1 = (f32[1,32,4096]{2,1,0:T(8,128)S(1)}, f32[1,32,4096]{2,1,0:T(8,128)S(1)}, u32[]{:S(2)}, u32[]{:S(2)}) collective-permute-start(f32[1,32,4096]{2,1,0:T(8,128)S(1)} %get-tuple-element.34), channel_id=1, source_target_pairs={{0,1},{1,2},{2,3},{3,4},{4,5},{5,6},{6,7},{7,8},{8,9},{9,10},{10,1... | collective-permute-start | bytes 1572872 | tf_op jit(solution)/shard_map/ppermute | solution.py:528
  11.4 1.1 %pack.5 = (f32[4,32,16384]{2,1,0:T(8,128)S(1)}, f32[1,32,4096]{2,1,0:T(8,128)S(1)}) custom-call(s32[8,256]{1,0:T(8,128)S(4)} %get-tuple-element.25.starts, f32[256,128]{1,0:T(8,128)S(1)} %get-tuple-element.26.flat, f32[4,32,16384]{2,1,0:T(8,128)S(1)} %get-tuple-element.32._, s32[256,128]{1,0:T(8,128)S(1)} %get-tuple-element.30.index), custom_call_target="tpu_custom_call", output_to_operand_aliasing={{0}: (2, {})} | custom-call | tf_op jit(solution)/shard_map/pack/pallas_call | solution.py:252
  12.5 0.1 collective-permute-start
  12.6 0.5 %collective-permute-start.4 = (f32[8,128]{1,0:T(8,128)S(1)}, f32[8,128]{1,0:T(8,128)S(1)}, u32[]{:S(2)}, u32[]{:S(2)}) collective-permute-start(f32[8,128]{1,0:T(8,128)S(1)} %get-tuple-element.43), channel_id=1, source_target_pairs={{0,1},{1,0},{2,3},{3,2},{4,5},{5,4},{6,7},{7,6},{8,9},{9,8},{10,11... | collective-permute-start | bytes 12296 | tf_op jit(solution)/shard_map/ppermute | solution.py:482
  13.1 1.4 %collective-permute-done.4.refs_0_ = f32[8,128]{1,0:T(8,128)S(1)} collective-permute-done((f32[8,128]{1,0:T(8,128)S(1)}, f32[8,128]{1,0:T(8,128)S(1)}, u32[]{:S(2)}, u32[]{:S(2)}) %collective-permute-start.4) | collective-permute-done | bytes 4128 | tf_op jit(solution)/shard_map/ppermute | solution.py:482
  14.5 1.3 %collective-permute-start.5 = (f32[8,128]{1,0:T(8,128)S(1)}, f32[8,128]{1,0:T(8,128)S(1)}, u32[]{:S(2)}, u32[]{:S(2)}) collective-permute-start(f32[8,128]{1,0:T(8,128)S(1)} %add.15.chip), channel_id=1, source_target_pairs={{0,9},{1,8},{2,11},{3,10},{4,13},{5,12},{6,15},{7,14},{8,1},{9,0},... | collective-permute-start | bytes 12296 | tf_op jit(solution)/shard_map/ppermute | solution.py:482
  15.8 2.0 %collective-permute-done.5.refs_2_ = f32[8,128]{1,0:T(8,128)S(1)} collective-permute-done((f32[8,128]{1,0:T(8,128)S(1)}, f32[8,128]{1,0:T(8,128)S(1)}, u32[]{:S(2)}, u32[]{:S(2)}) %collective-permute-start.5) | collective-permute-done | bytes 4128 | tf_op jit(solution)/shard_map/ppermute | solution.py:482
  17.8 2.9 %collective-permute-start.6 = (f32[8,128]{1,0:T(8,128)S(1)}, f32[8,128]{1,0:T(8,128)S(1)}, u32[]{:S(2)}, u32[]{:S(2)}) collective-permute-start(f32[8,128]{1,0:T(8,128)S(1)} %add.16), channel_id=1, source_target_pairs={{0,25},{1,24},{2,27},{3,26},{4,29},{5,28},{6,31},{7,30},{8,17},{9,... | collective-permute-start | bytes 12296 | tf_op jit(solution)/shard_map/ppermute | solution.py:482
  20.7 2.3 %collective-permute-done.6.refs_3_ = f32[8,128]{1,0:T(8,128)S(1)} collective-permute-done((f32[8,128]{1,0:T(8,128)S(1)}, f32[8,128]{1,0:T(8,128)S(1)}, u32[]{:S(2)}, u32[]{:S(2)}) %collective-permute-start.6) | collective-permute-done | bytes 4128 | tf_op jit(solution)/shard_map/ppermute | solution.py:482
  23.1 1.7 %collective-permute-start.7 = (f32[8,128]{1,0:T(8,128)S(1)}, f32[8,128]{1,0:T(8,128)S(1)}, u32[]{:S(2)}, u32[]{:S(2)}) collective-permute-start(f32[8,128]{1,0:T(8,128)S(1)} %add.17), channel_id=1, source_target_pairs={{0,33},{1,32},{2,35},{3,34},{4,37},{5,36},{6,39},{7,38},{8,41},{9,... | collective-permute-start | bytes 12296 | tf_op jit(solution)/shard_map/ppermute | solution.py:482
  24.8 1.6 %collective-permute-done.7.refs_0_ = f32[8,128]{1,0:T(8,128)S(1)} collective-permute-done((f32[8,128]{1,0:T(8,128)S(1)}, f32[8,128]{1,0:T(8,128)S(1)}, u32[]{:S(2)}, u32[]{:S(2)}) %collective-permute-start.7) | collective-permute-done | bytes 4128 | tf_op jit(solution)/shard_map/ppermute | solution.py:482
  26.4 4.0 %collective-permute-start.8 = (f32[8,128]{1,0:T(8,128)S(1)}, f32[8,128]{1,0:T(8,128)S(1)}, u32[]{:S(2)}, u32[]{:S(2)}) collective-permute-start(f32[8,128]{1,0:T(8,128)S(1)} %add.18), channel_id=1, source_target_pairs={{0,97},{1,96},{2,99},{3,98},{4,101},{5,100},{6,103},{7,102},{8,105... | collective-permute-start | bytes 12296 | tf_op jit(solution)/shard_map/ppermute | solution.py:482
  30.4 2.3 %collective-permute-done.8.refs_1_ = f32[8,128]{1,0:T(8,128)S(1)} collective-permute-done((f32[8,128]{1,0:T(8,128)S(1)}, f32[8,128]{1,0:T(8,128)S(1)}, u32[]{:S(2)}, u32[]{:S(2)}) %collective-permute-start.8) | collective-permute-done | bytes 4128 | tf_op jit(solution)/shard_map/ppermute | solution.py:482
  32.7 0.1 collective-permute-start.9
  32.7 2.7 %collective-permute-done.9.refs_1_ = f32[8,128]{1,0:T(8,128)S(1)} collective-permute-done((f32[8,128]{1,0:T(8,128)S(1)}, f32[8,128]{1,0:T(8,128)S(1)}, u32[]{:S(2)}, u32[]{:S(2)}) %collective-permute-start.9) | collective-permute-done | bytes 4128 | tf_op jit(solution)/shard_map/ppermute | solution.py:482
  35.5 1.5 %collective-permute-start.11 = (f32[8,128]{1,0:T(8,128)S(1)}, f32[8,128]{1,0:T(8,128)S(1)}, u32[]{:S(2)}, u32[]{:S(2)}) collective-permute-start(f32[8,128]{1,0:T(8,128)S(1)} %add.19), channel_id=1, source_target_pairs={{0,7},{1,6},{2,5},{3,0},{4,3},{5,2},{6,1},{7,4},{8,15},{9,14},{10,... | collective-permute-start | bytes 12296 | tf_op jit(solution)/shard_map/ppermute | solution.py:482
  37.0 2.8 %collective-permute-done.11.refs_3_ = f32[8,128]{1,0:T(8,128)S(1)} collective-permute-done((f32[8,128]{1,0:T(8,128)S(1)}, f32[8,128]{1,0:T(8,128)S(1)}, u32[]{:S(2)}, u32[]{:S(2)}) %collective-permute-start.11) | collective-permute-done | bytes 4128 | tf_op jit(solution)/shard_map/ppermute | solution.py:482
  39.7 0.0 collective-permute-start.10
  39.7 0.0 collective-permute-done.3.arrived
  39.7 0.5 %collective-permute-start.12 = (f32[8,128]{1,0:T(8,128)S(1)}, f32[8,128]{1,0:T(8,128)S(1)}, u32[]{:S(2)}, u32[]{:S(2)}) collective-permute-start(f32[8,128]{1,0:T(8,128)S(1)} %collective-permute-done.11.refs_3_), channel_id=1, source_target_pairs={{0,1},{1,0},{2,3},{3,2},{4,5},{5,4},{6,7},{7,6},{8,9},{9,8},{10,11... | collective-permute-start | bytes 12296 | tf_op jit(solution)/shard_map/ppermute | solution.py:482
  40.2 0.7 %spread.3._ = f32[4,32,16384]{2,1,0:T(8,128)S(1)} custom-call(s32[8,256]{1,0:T(8,128)S(4)} %get-tuple-element.25.starts, f32[1,32,4096]{2,1,0:T(8,128)S(1)} %collective-permute-done.3.arrived, f32[4,32,16384]{2,1,0:T(8,128)S(1)} %get-tuple-element.37._, s32[256,128]{1,0:T(8,128)S(1)} %get-tuple-element.38.ranks), custom_call_target="tpu_custom_call", output_to_operand_aliasing={{}: (2, {})} | custom-call | tf_op jit(solution)/shard_map/spread/pallas_call | solution.py:326
  40.9 1.1 %spread.4 = (f32[4,32,16384]{2,1,0:T(8,128)S(1)}, f32[4,32,8192]{2,1,0:T(8,128)}) custom-call(s32[8,256]{1,0:T(8,128)S(4)} %get-tuple-element.25.starts, f32[1,32,4096]{2,1,0:T(8,128)S(1)} %collective-permute-done.2.arrived, f32[4,32,16384]{2,1,0:T(8,128)S(1)} %spread.3._, s32[256,128]{1,0:T(8,128)S(1)} %get-tuple-element.38.ranks), custom_call_target="tpu_custom_call", output_to_operand_aliasing={{0}: (2, {})} | custom-call | tf_op jit(solution)/shard_map/spread/pallas_call | solution.py:326
  42.0 0.0 collective-permute-done.1.arrived
  42.0 1.1 %spread.5 = (f32[4,32,16384]{2,1,0:T(8,128)S(1)}, f32[4,32,8192]{2,1,0:T(8,128)}) custom-call(s32[8,256]{1,0:T(8,128)S(4)} %get-tuple-element.25.starts, f32[1,32,4096]{2,1,0:T(8,128)S(1)} %collective-permute-done.1.arrived, f32[4,32,16384]{2,1,0:T(8,128)S(1)} %get-tuple-element.39._, ...), custom_call_target="tpu_custom_call", output_to_operand_aliasing={{0}: (2, {}), {1}: (4, {})} | custom-call | tf_op jit(solution)/shard_map/spread/pallas_call | solution.py:326
  43.1 2.2 %deviate.1 = (f32[4,32,8192]{2,1,0:T(8,128)}, f32[4,32,8192]{2,1,0:T(8,128)}, f32[4,32,128]{2,1,0:T(8,128)S(1)}, f32[256,128]{1,0:T(8,128)S(1)}) custom-call(f32[4,32,16384]{2,1,0:T(8,128)S(1)} %get-tuple-element.41.state, s32[256,128]{1,0:T(8,128)S(1)} %get-tuple-element.38.ranks, ...), custom_call_target="tpu_custom_call", output_to_operand_aliasing={{0}: (2, {})} | custom-call | tf_op jit(solution)/shard_map/deviate/pallas_call | solution.py:413
  45.3 1.8 %finish.1 = (f32[4,32,8192]{2,1,0:T(8,128)}, f32[4,32,8192]{2,1,0:T(8,128)}) custom-call(s32[8,256]{1,0:T(8,128)S(4)} %get-tuple-element.25.starts, f32[1,32,4096]{2,1,0:T(8,128)S(1)} %collective-permute-done.arrived, f32[4,32,16384]{2,1,0:T(8,128)S(1)} %get-tuple-element.41.state, ...), custom_call_target="tpu_custom_call", output_to_operand_aliasing={{0}: (6, {}), {1}: (7, {})} | custom-call | tf_op jit(solution)/shard_map/finish/pallas_call | solution.py:461
  (10 shorter events, 0.0 us)
Async XLA Ops:
  4.3 35.5 %collective-permute-start.3 = (f32[1,32,4096]{2,1,0:T(8,128)S(1)}, f32[1,32,4096]{2,1,0:T(8,128)S(1)}, u32[]{:S(2)}, u32[]{:S(2)}) collective-permute-start(f32[1,32,4096]{2,1,0:T(8,128)S(1)} %get-tuple-element.36), channel_id=1, source_target_pairs={{0,1},{1,2},{2,3},{3,4},{4,5},{5,6},{6,7},{7,8},{8,9},{9,10},{10,1... | collective-permute-start | bytes 1572872 | tf_op jit(solution)/shard_map/ppermute | solution.py:528
  8.6 32.3 %collective-permute-start.2 = (f32[1,32,4096]{2,1,0:T(8,128)S(1)}, f32[1,32,4096]{2,1,0:T(8,128)S(1)}, u32[]{:S(2)}, u32[]{:S(2)}) collective-permute-start(f32[1,32,4096]{2,1,0:T(8,128)S(1)} %get-tuple-element.35), channel_id=1, source_target_pairs={{0,1},{1,2},{2,3},{3,4},{4,5},{5,6},{6,7},{7,8},{8,9},{9,10},{10,1... | collective-permute-start | bytes 1572872 | tf_op jit(solution)/shard_map/ppermute | solution.py:528
  9.8 32.2 %collective-permute-start.1 = (f32[1,32,4096]{2,1,0:T(8,128)S(1)}, f32[1,32,4096]{2,1,0:T(8,128)S(1)}, u32[]{:S(2)}, u32[]{:S(2)}) collective-permute-start(f32[1,32,4096]{2,1,0:T(8,128)S(1)} %get-tuple-element.34), channel_id=1, source_target_pairs={{0,1},{1,2},{2,3},{3,4},{4,5},{5,6},{6,7},{7,8},{8,9},{9,10},{10,1... | collective-permute-start | bytes 1572872 | tf_op jit(solution)/shard_map/ppermute | solution.py:528
  12.5 32.8 %collective-permute-start = (f32[1,32,4096]{2,1,0:T(8,128)S(1)}, f32[1,32,4096]{2,1,0:T(8,128)S(1)}, u32[]{:S(2)}, u32[]{:S(2)}) collective-permute-start(f32[1,32,4096]{2,1,0:T(8,128)S(1)} %get-tuple-element.33), channel_id=1, source_target_pairs={{0,1},{1,2},{2,3},{3,4},{4,5},{5,6},{6,7},{7,8},{8,9},{9,10},{10,1... | collective-permute-start | bytes 1572872 | tf_op jit(solution)/shard_map/ppermute | solution.py:528
  12.6 1.9 %collective-permute-start.4 = (f32[8,128]{1,0:T(8,128)S(1)}, f32[8,128]{1,0:T(8,128)S(1)}, u32[]{:S(2)}, u32[]{:S(2)}) collective-permute-start(f32[8,128]{1,0:T(8,128)S(1)} %get-tuple-element.43), channel_id=1, source_target_pairs={{0,1},{1,0},{2,3},{3,2},{4,5},{5,4},{6,7},{7,6},{8,9},{9,8},{10,11... | collective-permute-start | bytes 12296 | tf_op jit(solution)/shard_map/ppermute | solution.py:482
  14.5 3.3 %collective-permute-start.5 = (f32[8,128]{1,0:T(8,128)S(1)}, f32[8,128]{1,0:T(8,128)S(1)}, u32[]{:S(2)}, u32[]{:S(2)}) collective-permute-start(f32[8,128]{1,0:T(8,128)S(1)} %add.15.chip), channel_id=1, source_target_pairs={{0,9},{1,8},{2,11},{3,10},{4,13},{5,12},{6,15},{7,14},{8,1},{9,0},... | collective-permute-start | bytes 12296 | tf_op jit(solution)/shard_map/ppermute | solution.py:482
  17.8 5.2 %collective-permute-start.6 = (f32[8,128]{1,0:T(8,128)S(1)}, f32[8,128]{1,0:T(8,128)S(1)}, u32[]{:S(2)}, u32[]{:S(2)}) collective-permute-start(f32[8,128]{1,0:T(8,128)S(1)} %add.16), channel_id=1, source_target_pairs={{0,25},{1,24},{2,27},{3,26},{4,29},{5,28},{6,31},{7,30},{8,17},{9,... | collective-permute-start | bytes 12296 | tf_op jit(solution)/shard_map/ppermute | solution.py:482
  23.1 3.3 %collective-permute-start.7 = (f32[8,128]{1,0:T(8,128)S(1)}, f32[8,128]{1,0:T(8,128)S(1)}, u32[]{:S(2)}, u32[]{:S(2)}) collective-permute-start(f32[8,128]{1,0:T(8,128)S(1)} %add.17), channel_id=1, source_target_pairs={{0,33},{1,32},{2,35},{3,34},{4,37},{5,36},{6,39},{7,38},{8,41},{9,... | collective-permute-start | bytes 12296 | tf_op jit(solution)/shard_map/ppermute | solution.py:482
  26.4 6.3 %collective-permute-start.8 = (f32[8,128]{1,0:T(8,128)S(1)}, f32[8,128]{1,0:T(8,128)S(1)}, u32[]{:S(2)}, u32[]{:S(2)}) collective-permute-start(f32[8,128]{1,0:T(8,128)S(1)} %add.18), channel_id=1, source_target_pairs={{0,97},{1,96},{2,99},{3,98},{4,101},{5,100},{6,103},{7,102},{8,105... | collective-permute-start | bytes 12296 | tf_op jit(solution)/shard_map/ppermute | solution.py:482
  32.7 2.8 %collective-permute-start.9 = (f32[8,128]{1,0:T(8,128)S(1)}, f32[8,128]{1,0:T(8,128)S(1)}, u32[]{:S(2)}, u32[]{:S(2)}) collective-permute-start(f32[8,128]{1,0:T(8,128)S(1)} %between.1.own), channel_id=1, source_target_pairs={{0,2},{1,7},{2,0},{3,1},{4,6},{5,3},{6,4},{7,5},{8,10},{9,15},{10,... | collective-permute-start | bytes 12296 | tf_op jit(solution)/shard_map/ppermute | solution.py:482
  35.5 4.2 %collective-permute-start.11 = (f32[8,128]{1,0:T(8,128)S(1)}, f32[8,128]{1,0:T(8,128)S(1)}, u32[]{:S(2)}, u32[]{:S(2)}) collective-permute-start(f32[8,128]{1,0:T(8,128)S(1)} %add.19), channel_id=1, source_target_pairs={{0,7},{1,6},{2,5},{3,0},{4,3},{5,2},{6,1},{7,4},{8,15},{9,14},{10,... | collective-permute-start | bytes 12296 | tf_op jit(solution)/shard_map/ppermute | solution.py:482
  39.7 3.4 %collective-permute-start.10 = (f32[8,128]{1,0:T(8,128)S(1)}, f32[8,128]{1,0:T(8,128)S(1)}, u32[]{:S(2)}, u32[]{:S(2)}) collective-permute-start(f32[8,128]{1,0:T(8,128)S(1)} %collective-permute-done.9.refs_1_), channel_id=1, source_target_pairs={{0,1},{1,0},{2,3},{3,2},{4,5},{5,4},{6,7},{7,6},{8,9},{9,8},{10,11... | collective-permute-start | bytes 12296 | tf_op jit(solution)/shard_map/ppermute | solution.py:482
  39.7 3.4 %collective-permute-start.12 = (f32[8,128]{1,0:T(8,128)S(1)}, f32[8,128]{1,0:T(8,128)S(1)}, u32[]{:S(2)}, u32[]{:S(2)}) collective-permute-start(f32[8,128]{1,0:T(8,128)S(1)} %collective-permute-done.11.refs_3_), channel_id=1, source_target_pairs={{0,1},{1,0},{2,3},{3,2},{4,5},{5,4},{6,7},{7,6},{8,9},{9,8},{10,11... | collective-permute-start | bytes 12296 | tf_op jit(solution)/shard_map/ppermute | solution.py:482

commit v4 on v3

--- a/solution.py
+++ b/solution.py
@@ -13,7 +13,7 @@
 LANES = 128
 GROUP = 64
 GROUP_SUM = 16
-PARTS = 2
+PARTS = 4
 ROWS = ("rows_0", "rows_1", "rows_2", "rows_3")
 SHAPE = (4, 4, 4, 2)
 F32 = jnp.float32
@@ -35,24 +35,27 @@
     return ((row <= column) | (column >= LANES)).astype(F32).astype(BF16)
 
 
-def index_tables(keep, flat, scalars, copy, streams, tiles):
+def index_tables(keep, flags_in, loads, masks, flat, scalars, copy, streams, tiles):
     count = streams * tiles
+    row = lax.broadcasted_iota(I32, (count, count), 0)
+    column = lax.broadcasted_iota(I32, (count, count), 1)
+    same = ((row ^ column) & (streams - 1)) == 0
+    masks[0] = (same & (column < row)).astype(F32).astype(BF16)
+    masks[1] = (same & (column > row)).astype(F32).astype(BF16)
+    flags_in.wait()
+    for load in loads:
+        load.start()
     for t in range(tiles):
         flat[t * streams : (t + 1) * streams, :] = keep[:, t * LANES : (t + 1) * LANES].astype(F32)
     flags = flat[...].astype(BF16)
     weights = running_weights()[:LANES]
     sums = jnp.dot(flags, weights, preferred_element_type=F32)
     within, total = (sums[:, :LANES], sums[:, LANES:])
-    row = lax.broadcasted_iota(I32, (count, count), 0)
-    column = lax.broadcasted_iota(I32, (count, count), 1)
-    same = ((row ^ column) & (streams - 1)) == 0
-    earlier = (same & (column < row)).astype(F32).astype(BF16)
-    later = (same & (column > row)).astype(F32).astype(BF16)
-    start = jnp.dot(earlier, total.astype(BF16), preferred_element_type=F32)
+    start = jnp.dot(masks[0], total.astype(BF16), preferred_element_type=F32)
     line = lax.dot_general(
         jnp.ones((8, LANES), BF16), flags, (((1,), (1,)), ((), ())), preferred_element_type=F32
     )
-    line_start = jnp.dot(line.astype(BF16), later, preferred_element_type=F32)
+    line_start = jnp.dot(line.astype(BF16), masks[1], preferred_element_type=F32)
     sublane = lax.broadcasted_iota(I32, (8, count), 0)
     base = line_start + jnp.where(line == float(LANES), 1.0, 0.0)
     table = jnp.where(sublane == 0, line_start, jnp.where(sublane == 1, base, line_start + line))
@@ -60,7 +63,7 @@
     copy.start()
     ordinal = lanes_of(count).astype(F32)
     place = jnp.zeros((count, LANES), I32)
-    for step, times in ((32, 3), (8, 3), (2, 3), (1, 1)):
+    for step, times in ((64, 1), (32, 1), (16, 1), (8, 1), (4, 1), (2, 1), (1, 1)):
         found = place
         for k in range(1, times + 1):
             seen = picked_lanes(within, place + (k * step - 1))
@@ -134,7 +137,7 @@
 
 def pack_first_body(
     keep_hbm, events, state, flat, index, ranks, starts, tail, totals,
-    keep, scalars, work, copied, loaded,
+    keep, scalars, masks, work, copied, published, loaded,
 ):
     streams, length = keep.shape
     tiles = length // LANES
@@ -145,11 +148,10 @@
     flags = pltpu.make_async_copy(keep_hbm, keep, copied)
     flags.start()
     loads[0].start()
-    flags.wait()
-    for load in loads[1:]:
-        load.start()
-    copy = pltpu.make_async_copy(scalars, starts, copied)
-    index[...], ranks[...] = index_tables(keep, flat, scalars, copy, streams, tiles)
+    copy = pltpu.make_async_copy(scalars, starts, published)
+    index[...], ranks[...] = index_tables(
+        keep, flags, loads[1:], masks, flat, scalars, copy, streams, tiles
+    )
     copy.wait()
     loads[0].wait()
     total = pack_stream(
@@ -228,7 +230,9 @@
         scratch_shapes=[
             pltpu.VMEM((streams, length), I32),
             pltpu.VMEM((8, count), I32),
+            pltpu.VMEM((2, count, count), BF16),
             pltpu.VMEM((features, length + LANES), F32),
+            pltpu.SemaphoreType.DMA,
             pltpu.SemaphoreType.DMA,
             pltpu.SemaphoreType.DMA((streams,)),
         ],

time: 47.4 us -> 47 us (level)
  no operation moved by 1% of the time
where the time goes in v4:
time: 47 us; the launch traced here: 46.9 us
  starting transfers between devices  16.9 us (36%)
  waiting for transfers between devices  15.2 us (32%)
  Pallas kernels  14 us (30%)
  between operations  0.76 us (2%)
    ppermute x9, waiting for transfers between devices, permuted(): lax.ppermute(value, ROWS, [(number[place], number[target(*place)]) for pl...  15.2 us
    ppermute x9, starting transfers between devices, permuted(): lax.ppermute(value, ROWS, [(number[place], number[target(*place)]) for pl...  12.4 us
    ppermute x4, starting transfers between devices, from_behind(): lax.ppermute(value, ROWS, [(k, (k + 1) % count) for k in range(count)])  4.5 us
    pallas_call x1, Pallas kernels, pack_first(): pl.pallas_call(pack_first_body, in_specs=[IN_HBM, IN_HBM], out_specs=[IN_...  3.51 us
    pallas_call x3, Pallas kernels, pack(): pl.pallas_call(body, in_specs=[IN_SMEM] + [IN_VMEM] * (3 + len(given)), o...  3.26 us
    pallas_call x3, Pallas kernels, spread(): pl.pallas_call(body, in_specs=[IN_SMEM] + [IN_VMEM] * 3 + [IN_HBM] * len(...  2.8 us
    pallas_call x1, Pallas kernels, deviate(): pl.pallas_call(body, in_specs=[IN_VMEM] * 2 + [IN_HBM] + [IN_VMEM] * (1 +...  2.2 us
    pallas_call x1, Pallas kernels, finish(): pl.pallas_call(body, in_specs=[IN_SMEM] + [IN_VMEM] * 5 + [IN_HBM] * 2, o...  1.67 us
  transfers between devices with their start and end apart: 13, of which 7 were waited for; matrix products, arithmetic and copies ran while one was open for 0% of the time, Pallas kernels for 19%

profile of v4, /device:TPU:1, one launch (start us, length us, event | category | flops | bytes accessed | tf_op | source)
XLA Modules:
  0.0 46.9 jit_solution(14140669586955735542)
XLA Ops:
  0.6 3.5 %pack_first.1 = (f32[4,32,16384]{2,1,0:T(8,128)S(1)}, f32[256,128]{1,0:T(8,128)S(1)}, s32[256,128]{1,0:T(8,128)S(1)}, s32[256,128]{1,0:T(8,128)S(1)}, s32[8,256]...) custom-call(s32[4,8192]{1,0:T(4,128)} %keep_hbm.1, f32[4,32,8192]{2,1,0:T(8,128)} %events.1), custom_call_target="tpu_custom_call" | custom-call | tf_op jit(solution)/shard_map/pack_first/pallas_call | solution.py:225
  4.1 2.7 %collective-permute-start.3 = (f32[1,32,4096]{2,1,0:T(8,128)S(1)}, f32[1,32,4096]{2,1,0:T(8,128)S(1)}, u32[]{:S(2)}, u32[]{:S(2)}) collective-permute-start(f32[1,32,4096]{2,1,0:T(8,128)S(1)} %get-tuple-element.36), channel_id=1, source_target_pairs={{0,1},{1,2},{2,3},{3,4},{4,5},{5,6},{6,7},{7,8},{8,9},{9,10},{10,1... | collective-permute-start | bytes 1572872 | tf_op jit(solution)/shard_map/ppermute | solution.py:532
  6.8 0.5 %add_totals.1 = (f32[4,32,16384]{2,1,0:T(8,128)S(1)}, f32[8,128]{1,0:T(8,128)S(1)}) custom-call(f32[256,128]{1,0:T(8,128)S(1)} %get-tuple-element.26.flat, f32[4,32,16384]{2,1,0:T(8,128)S(1)} %get-tuple-element.27._, f32[8,128]{1,0:T(8,128)S(1)} %get-tuple-element.28.so_far), custom_call_target="tpu_custom_call", output_to_operand_aliasing={{0}: (1, {})} | custom-call | tf_op jit(solution)/shard_map/add_totals/pallas_call | solution.py:298
  7.4 1.1 %pack.3 = (f32[4,32,16384]{2,1,0:T(8,128)S(1)}, f32[1,32,4096]{2,1,0:T(8,128)S(1)}) custom-call(s32[8,256]{1,0:T(8,128)S(4)} %get-tuple-element.25.starts, f32[256,128]{1,0:T(8,128)S(1)} %get-tuple-element.26.flat, f32[4,32,16384]{2,1,0:T(8,128)S(1)} %get-tuple-element.29._, s32[256,128]{1,0:T(8,128)S(1)} %get-tuple-element.30.index), custom_call_target="tpu_custom_call", output_to_operand_aliasing={{0}: (2, {})} | custom-call | tf_op jit(solution)/shard_map/pack/pallas_call | solution.py:256
  8.5 0.1 collective-permute-start.2
  8.5 1.1 %pack.4 = (f32[4,32,16384]{2,1,0:T(8,128)S(1)}, f32[1,32,4096]{2,1,0:T(8,128)S(1)}) custom-call(s32[8,256]{1,0:T(8,128)S(4)} %get-tuple-element.25.starts, f32[256,128]{1,0:T(8,128)S(1)} %get-tuple-element.26.flat, f32[4,32,16384]{2,1,0:T(8,128)S(1)} %get-tuple-element.31._, s32[256,128]{1,0:T(8,128)S(1)} %get-tuple-element.30.index), custom_call_target="tpu_custom_call", output_to_operand_aliasing={{0}: (2, {})} | custom-call | tf_op jit(solution)/shard_map/pack/pallas_call | solution.py:256
  9.6 1.7 %collective-permute-start.1 = (f32[1,32,4096]{2,1,0:T(8,128)S(1)}, f32[1,32,4096]{2,1,0:T(8,128)S(1)}, u32[]{:S(2)}, u32[]{:S(2)}) collective-permute-start(f32[1,32,4096]{2,1,0:T(8,128)S(1)} %get-tuple-element.34), channel_id=1, source_target_pairs={{0,1},{1,2},{2,3},{3,4},{4,5},{5,6},{6,7},{7,8},{8,9},{9,10},{10,1... | collective-permute-start | bytes 1572872 | tf_op jit(solution)/shard_map/ppermute | solution.py:532
  11.3 1.1 %pack.5 = (f32[4,32,16384]{2,1,0:T(8,128)S(1)}, f32[1,32,4096]{2,1,0:T(8,128)S(1)}) custom-call(s32[8,256]{1,0:T(8,128)S(4)} %get-tuple-element.25.starts, f32[256,128]{1,0:T(8,128)S(1)} %get-tuple-element.26.flat, f32[4,32,16384]{2,1,0:T(8,128)S(1)} %get-tuple-element.32._, s32[256,128]{1,0:T(8,128)S(1)} %get-tuple-element.30.index), custom_call_target="tpu_custom_call", output_to_operand_aliasing={{0}: (2, {})} | custom-call | tf_op jit(solution)/shard_map/pack/pallas_call | solution.py:256
  12.4 0.1 collective-permute-start
  12.5 0.5 %collective-permute-start.4 = (f32[8,128]{1,0:T(8,128)S(1)}, f32[8,128]{1,0:T(8,128)S(1)}, u32[]{:S(2)}, u32[]{:S(2)}) collective-permute-start(f32[8,128]{1,0:T(8,128)S(1)} %get-tuple-element.43), channel_id=1, source_target_pairs={{0,1},{1,0},{2,3},{3,2},{4,5},{5,4},{6,7},{7,6},{8,9},{9,8},{10,11... | collective-permute-start | bytes 12296 | tf_op jit(solution)/shard_map/ppermute | solution.py:486
  13.0 1.4 %collective-permute-done.4.refs_0_ = f32[8,128]{1,0:T(8,128)S(1)} collective-permute-done((f32[8,128]{1,0:T(8,128)S(1)}, f32[8,128]{1,0:T(8,128)S(1)}, u32[]{:S(2)}, u32[]{:S(2)}) %collective-permute-start.4) | collective-permute-done | bytes 4128 | tf_op jit(solution)/shard_map/ppermute | solution.py:486
  14.4 1.3 %collective-permute-start.5 = (f32[8,128]{1,0:T(8,128)S(1)}, f32[8,128]{1,0:T(8,128)S(1)}, u32[]{:S(2)}, u32[]{:S(2)}) collective-permute-start(f32[8,128]{1,0:T(8,128)S(1)} %add.15.chip), channel_id=1, source_target_pairs={{0,9},{1,8},{2,11},{3,10},{4,13},{5,12},{6,15},{7,14},{8,1},{9,0},... | collective-permute-start | bytes 12296 | tf_op jit(solution)/shard_map/ppermute | solution.py:486
  15.7 2.0 %collective-permute-done.5.refs_2_ = f32[8,128]{1,0:T(8,128)S(1)} collective-permute-done((f32[8,128]{1,0:T(8,128)S(1)}, f32[8,128]{1,0:T(8,128)S(1)}, u32[]{:S(2)}, u32[]{:S(2)}) %collective-permute-start.5) | collective-permute-done | bytes 4128 | tf_op jit(solution)/shard_map/ppermute | solution.py:486
  17.7 2.9 %collective-permute-start.6 = (f32[8,128]{1,0:T(8,128)S(1)}, f32[8,128]{1,0:T(8,128)S(1)}, u32[]{:S(2)}, u32[]{:S(2)}) collective-permute-start(f32[8,128]{1,0:T(8,128)S(1)} %add.16), channel_id=1, source_target_pairs={{0,25},{1,24},{2,27},{3,26},{4,29},{5,28},{6,31},{7,30},{8,17},{9,... | collective-permute-start | bytes 12296 | tf_op jit(solution)/shard_map/ppermute | solution.py:486
  20.6 2.3 %collective-permute-done.6.refs_3_ = f32[8,128]{1,0:T(8,128)S(1)} collective-permute-done((f32[8,128]{1,0:T(8,128)S(1)}, f32[8,128]{1,0:T(8,128)S(1)}, u32[]{:S(2)}, u32[]{:S(2)}) %collective-permute-start.6) | collective-permute-done | bytes 4128 | tf_op jit(solution)/shard_map/ppermute | solution.py:486
  22.9 1.7 %collective-permute-start.7 = (f32[8,128]{1,0:T(8,128)S(1)}, f32[8,128]{1,0:T(8,128)S(1)}, u32[]{:S(2)}, u32[]{:S(2)}) collective-permute-start(f32[8,128]{1,0:T(8,128)S(1)} %add.17), channel_id=1, source_target_pairs={{0,33},{1,32},{2,35},{3,34},{4,37},{5,36},{6,39},{7,38},{8,41},{9,... | collective-permute-start | bytes 12296 | tf_op jit(solution)/shard_map/ppermute | solution.py:486
  24.7 1.6 %collective-permute-done.7.refs_0_ = f32[8,128]{1,0:T(8,128)S(1)} collective-permute-done((f32[8,128]{1,0:T(8,128)S(1)}, f32[8,128]{1,0:T(8,128)S(1)}, u32[]{:S(2)}, u32[]{:S(2)}) %collective-permute-start.7) | collective-permute-done | bytes 4128 | tf_op jit(solution)/shard_map/ppermute | solution.py:486
  26.3 4.0 %collective-permute-start.8 = (f32[8,128]{1,0:T(8,128)S(1)}, f32[8,128]{1,0:T(8,128)S(1)}, u32[]{:S(2)}, u32[]{:S(2)}) collective-permute-start(f32[8,128]{1,0:T(8,128)S(1)} %add.18), channel_id=1, source_target_pairs={{0,97},{1,96},{2,99},{3,98},{4,101},{5,100},{6,103},{7,102},{8,105... | collective-permute-start | bytes 12296 | tf_op jit(solution)/shard_map/ppermute | solution.py:486
  30.2 2.3 %collective-permute-done.8.refs_1_ = f32[8,128]{1,0:T(8,128)S(1)} collective-permute-done((f32[8,128]{1,0:T(8,128)S(1)}, f32[8,128]{1,0:T(8,128)S(1)}, u32[]{:S(2)}, u32[]{:S(2)}) %collective-permute-start.8) | collective-permute-done | bytes 4128 | tf_op jit(solution)/shard_map/ppermute | solution.py:486
  32.5 0.1 collective-permute-start.9
  32.6 2.7 %collective-permute-done.9.refs_1_ = f32[8,128]{1,0:T(8,128)S(1)} collective-permute-done((f32[8,128]{1,0:T(8,128)S(1)}, f32[8,128]{1,0:T(8,128)S(1)}, u32[]{:S(2)}, u32[]{:S(2)}) %collective-permute-start.9) | collective-permute-done | bytes 4128 | tf_op jit(solution)/shard_map/ppermute | solution.py:486
  35.4 1.5 %collective-permute-start.11 = (f32[8,128]{1,0:T(8,128)S(1)}, f32[8,128]{1,0:T(8,128)S(1)}, u32[]{:S(2)}, u32[]{:S(2)}) collective-permute-start(f32[8,128]{1,0:T(8,128)S(1)} %add.19), channel_id=1, source_target_pairs={{0,7},{1,6},{2,5},{3,0},{4,3},{5,2},{6,1},{7,4},{8,15},{9,14},{10,... | collective-permute-start | bytes 12296 | tf_op jit(solution)/shard_map/ppermute | solution.py:486
  36.8 2.8 %collective-permute-done.11.refs_3_ = f32[8,128]{1,0:T(8,128)S(1)} collective-permute-done((f32[8,128]{1,0:T(8,128)S(1)}, f32[8,128]{1,0:T(8,128)S(1)}, u32[]{:S(2)}, u32[]{:S(2)}) %collective-permute-start.11) | collective-permute-done | bytes 4128 | tf_op jit(solution)/shard_map/ppermute | solution.py:486
  39.6 0.0 collective-permute-done.3.arrived
  39.6 0.5 %collective-permute-start.12 = (f32[8,128]{1,0:T(8,128)S(1)}, f32[8,128]{1,0:T(8,128)S(1)}, u32[]{:S(2)}, u32[]{:S(2)}) collective-permute-start(f32[8,128]{1,0:T(8,128)S(1)} %collective-permute-done.11.refs_3_), channel_id=1, source_target_pairs={{0,1},{1,0},{2,3},{3,2},{4,5},{5,4},{6,7},{7,6},{8,9},{9,8},{10,11... | collective-permute-start | bytes 12296 | tf_op jit(solution)/shard_map/ppermute | solution.py:486
  40.1 0.7 %spread.3._ = f32[4,32,16384]{2,1,0:T(8,128)S(1)} custom-call(s32[8,256]{1,0:T(8,128)S(4)} %get-tuple-element.25.starts, f32[1,32,4096]{2,1,0:T(8,128)S(1)} %collective-permute-done.3.arrived, f32[4,32,16384]{2,1,0:T(8,128)S(1)} %get-tuple-element.37._, s32[256,128]{1,0:T(8,128)S(1)} %get-tuple-element.38.ranks), custom_call_target="tpu_custom_call", output_to_operand_aliasing={{}: (2, {})} | custom-call | tf_op jit(solution)/shard_map/spread/pallas_call | solution.py:330
  40.8 0.0 collective-permute-done.2.arrived
  40.8 1.1 %spread.4 = (f32[4,32,16384]{2,1,0:T(8,128)S(1)}, f32[4,32,8192]{2,1,0:T(8,128)}) custom-call(s32[8,256]{1,0:T(8,128)S(4)} %get-tuple-element.25.starts, f32[1,32,4096]{2,1,0:T(8,128)S(1)} %collective-permute-done.2.arrived, f32[4,32,16384]{2,1,0:T(8,128)S(1)} %spread.3._, s32[256,128]{1,0:T(8,128)S(1)} %get-tuple-element.38.ranks), custom_call_target="tpu_custom_call", output_to_operand_aliasing={{0}: (2, {})} | custom-call | tf_op jit(solution)/shard_map/spread/pallas_call | solution.py:330
  41.9 0.0 collective-permute-done.1.arrived
  41.9 1.1 %spread.5 = (f32[4,32,16384]{2,1,0:T(8,128)S(1)}, f32[4,32,8192]{2,1,0:T(8,128)}) custom-call(s32[8,256]{1,0:T(8,128)S(4)} %get-tuple-element.25.starts, f32[1,32,4096]{2,1,0:T(8,128)S(1)} %collective-permute-done.1.arrived, f32[4,32,16384]{2,1,0:T(8,128)S(1)} %get-tuple-element.39._, ...), custom_call_target="tpu_custom_call", output_to_operand_aliasing={{0}: (2, {}), {1}: (4, {})} | custom-call | tf_op jit(solution)/shard_map/spread/pallas_call | solution.py:330
  43.0 2.2 %deviate.1 = (f32[4,32,8192]{2,1,0:T(8,128)}, f32[4,32,8192]{2,1,0:T(8,128)}, f32[4,32,128]{2,1,0:T(8,128)S(1)}, f32[256,128]{1,0:T(8,128)S(1)}) custom-call(f32[4,32,16384]{2,1,0:T(8,128)S(1)} %get-tuple-element.41.state, s32[256,128]{1,0:T(8,128)S(1)} %get-tuple-element.38.ranks, ...), custom_call_target="tpu_custom_call", output_to_operand_aliasing={{0}: (2, {})} | custom-call | tf_op jit(solution)/shard_map/deviate/pallas_call | solution.py:417
  45.2 1.7 %finish.1 = (f32[4,32,8192]{2,1,0:T(8,128)}, f32[4,32,8192]{2,1,0:T(8,128)}) custom-call(s32[8,256]{1,0:T(8,128)S(4)} %get-tuple-element.25.starts, f32[1,32,4096]{2,1,0:T(8,128)S(1)} %collective-permute-done.arrived, f32[4,32,16384]{2,1,0:T(8,128)S(1)} %get-tuple-element.41.state, ...), custom_call_target="tpu_custom_call", output_to_operand_aliasing={{0}: (6, {}), {1}: (7, {})} | custom-call | tf_op jit(solution)/shard_map/finish/pallas_call | solution.py:465
  (10 shorter events, 0.0 us)
Async XLA Ops:
  4.1 35.5 %collective-permute-start.3 = (f32[1,32,4096]{2,1,0:T(8,128)S(1)}, f32[1,32,4096]{2,1,0:T(8,128)S(1)}, u32[]{:S(2)}, u32[]{:S(2)}) collective-permute-start(f32[1,32,4096]{2,1,0:T(8,128)S(1)} %get-tuple-element.36), channel_id=1, source_target_pairs={{0,1},{1,2},{2,3},{3,4},{4,5},{5,6},{6,7},{7,8},{8,9},{9,10},{10,1... | collective-permute-start | bytes 1572872 | tf_op jit(solution)/shard_map/ppermute | solution.py:532
  8.5 32.3 %collective-permute-start.2 = (f32[1,32,4096]{2,1,0:T(8,128)S(1)}, f32[1,32,4096]{2,1,0:T(8,128)S(1)}, u32[]{:S(2)}, u32[]{:S(2)}) collective-permute-start(f32[1,32,4096]{2,1,0:T(8,128)S(1)} %get-tuple-element.35), channel_id=1, source_target_pairs={{0,1},{1,2},{2,3},{3,4},{4,5},{5,6},{6,7},{7,8},{8,9},{9,10},{10,1... | collective-permute-start | bytes 1572872 | tf_op jit(solution)/shard_map/ppermute | solution.py:532
  9.6 32.2 %collective-permute-start.1 = (f32[1,32,4096]{2,1,0:T(8,128)S(1)}, f32[1,32,4096]{2,1,0:T(8,128)S(1)}, u32[]{:S(2)}, u32[]{:S(2)}) collective-permute-start(f32[1,32,4096]{2,1,0:T(8,128)S(1)} %get-tuple-element.34), channel_id=1, source_target_pairs={{0,1},{1,2},{2,3},{3,4},{4,5},{5,6},{6,7},{7,8},{8,9},{9,10},{10,1... | collective-permute-start | bytes 1572872 | tf_op jit(solution)/shard_map/ppermute | solution.py:532
  12.4 32.8 %collective-permute-start = (f32[1,32,4096]{2,1,0:T(8,128)S(1)}, f32[1,32,4096]{2,1,0:T(8,128)S(1)}, u32[]{:S(2)}, u32[]{:S(2)}) collective-permute-start(f32[1,32,4096]{2,1,0:T(8,128)S(1)} %get-tuple-element.33), channel_id=1, source_target_pairs={{0,1},{1,2},{2,3},{3,4},{4,5},{5,6},{6,7},{7,8},{8,9},{9,10},{10,1... | collective-permute-start | bytes 1572872 | tf_op jit(solution)/shard_map/ppermute | solution.py:532
  12.5 1.9 %collective-permute-start.4 = (f32[8,128]{1,0:T(8,128)S(1)}, f32[8,128]{1,0:T(8,128)S(1)}, u32[]{:S(2)}, u32[]{:S(2)}) collective-permute-start(f32[8,128]{1,0:T(8,128)S(1)} %get-tuple-element.43), channel_id=1, source_target_pairs={{0,1},{1,0},{2,3},{3,2},{4,5},{5,4},{6,7},{7,6},{8,9},{9,8},{10,11... | collective-permute-start | bytes 12296 | tf_op jit(solution)/shard_map/ppermute | solution.py:486
  14.4 3.3 %collective-permute-start.5 = (f32[8,128]{1,0:T(8,128)S(1)}, f32[8,128]{1,0:T(8,128)S(1)}, u32[]{:S(2)}, u32[]{:S(2)}) collective-permute-start(f32[8,128]{1,0:T(8,128)S(1)} %add.15.chip), channel_id=1, source_target_pairs={{0,9},{1,8},{2,11},{3,10},{4,13},{5,12},{6,15},{7,14},{8,1},{9,0},... | collective-permute-start | bytes 12296 | tf_op jit(solution)/shard_map/ppermute | solution.py:486
  17.7 5.2 %collective-permute-start.6 = (f32[8,128]{1,0:T(8,128)S(1)}, f32[8,128]{1,0:T(8,128)S(1)}, u32[]{:S(2)}, u32[]{:S(2)}) collective-permute-start(f32[8,128]{1,0:T(8,128)S(1)} %add.16), channel_id=1, source_target_pairs={{0,25},{1,24},{2,27},{3,26},{4,29},{5,28},{6,31},{7,30},{8,17},{9,... | collective-permute-start | bytes 12296 | tf_op jit(solution)/shard_map/ppermute | solution.py:486
  22.9 3.3 %collective-permute-start.7 = (f32[8,128]{1,0:T(8,128)S(1)}, f32[8,128]{1,0:T(8,128)S(1)}, u32[]{:S(2)}, u32[]{:S(2)}) collective-permute-start(f32[8,128]{1,0:T(8,128)S(1)} %add.17), channel_id=1, source_target_pairs={{0,33},{1,32},{2,35},{3,34},{4,37},{5,36},{6,39},{7,38},{8,41},{9,... | collective-permute-start | bytes 12296 | tf_op jit(solution)/shard_map/ppermute | solution.py:486
  26.3 6.3 %collective-permute-start.8 = (f32[8,128]{1,0:T(8,128)S(1)}, f32[8,128]{1,0:T(8,128)S(1)}, u32[]{:S(2)}, u32[]{:S(2)}) collective-permute-start(f32[8,128]{1,0:T(8,128)S(1)} %add.18), channel_id=1, source_target_pairs={{0,97},{1,96},{2,99},{3,98},{4,101},{5,100},{6,103},{7,102},{8,105... | collective-permute-start | bytes 12296 | tf_op jit(solution)/shard_map/ppermute | solution.py:486
  32.5 2.8 %collective-permute-start.9 = (f32[8,128]{1,0:T(8,128)S(1)}, f32[8,128]{1,0:T(8,128)S(1)}, u32[]{:S(2)}, u32[]{:S(2)}) collective-permute-start(f32[8,128]{1,0:T(8,128)S(1)} %between.1.own), channel_id=1, source_target_pairs={{0,2},{1,7},{2,0},{3,1},{4,6},{5,3},{6,4},{7,5},{8,10},{9,15},{10,... | collective-permute-start | bytes 12296 | tf_op jit(solution)/shard_map/ppermute | solution.py:486
  35.4 4.2 %collective-permute-start.11 = (f32[8,128]{1,0:T(8,128)S(1)}, f32[8,128]{1,0:T(8,128)S(1)}, u32[]{:S(2)}, u32[]{:S(2)}) collective-permute-start(f32[8,128]{1,0:T(8,128)S(1)} %add.19), channel_id=1, source_target_pairs={{0,7},{1,6},{2,5},{3,0},{4,3},{5,2},{6,1},{7,4},{8,15},{9,14},{10,... | collective-permute-start | bytes 12296 | tf_op jit(solution)/shard_map/ppermute | solution.py:486
  39.6 3.4 %collective-permute-start.10 = (f32[8,128]{1,0:T(8,128)S(1)}, f32[8,128]{1,0:T(8,128)S(1)}, u32[]{:S(2)}, u32[]{:S(2)}) collective-permute-start(f32[8,128]{1,0:T(8,128)S(1)} %collective-permute-done.9.refs_1_), channel_id=1, source_target_pairs={{0,1},{1,0},{2,3},{3,2},{4,5},{5,4},{6,7},{7,6},{8,9},{9,8},{10,11... | collective-permute-start | bytes 12296 | tf_op jit(solution)/shard_map/ppermute | solution.py:486
  39.6 3.4 %collective-permute-start.12 = (f32[8,128]{1,0:T(8,128)S(1)}, f32[8,128]{1,0:T(8,128)S(1)}, u32[]{:S(2)}, u32[]{:S(2)}) collective-permute-start(f32[8,128]{1,0:T(8,128)S(1)} %collective-permute-done.11.refs_3_), channel_id=1, source_target_pairs={{0,1},{1,0},{2,3},{3,2},{4,5},{5,4},{6,7},{7,6},{8,9},{9,8},{10,11... | collective-permute-start | bytes 12296 | tf_op jit(solution)/shard_map/ppermute | solution.py:486
